TPU v7x, 128 devices: a whole 4x4x4 slice. The times are simulated.
128 devices in a mesh: batch: 1, col: 2 (over core), row: 64 (over z, y, x).
Axes of the slice: x: 4, y: 4, z: 4, core: 2. Of those that a mesh axis runs over, the one named last changes fastest.
Arguments:
- images: bfloat16 [16, 512, 128, 128], P('batch', 'row', 'col')
- w_down1: bfloat16 [4, 4, 128, 256], replicated
- b_down1: float32 [256], replicated
- w_conv1: bfloat16 [3, 3, 256, 256], replicated
- b_conv1: float32 [256], replicated
- w_down2: bfloat16 [4, 4, 256, 256], replicated
- b_down2: float32 [256], replicated
- w_conv2: bfloat16 [3, 3, 256, 256], replicated
- b_conv2: float32 [256], replicated
- w_down3: bfloat16 [4, 4, 256, 256], replicated
- b_down3: float32 [256], replicated
- w_conv3: bfloat16 [3, 3, 256, 256], replicated
- b_conv3: float32 [256], replicated
Outputs:
- output: bfloat16 [16, 64, 16, 256], P('batch', 'row', 'col')
All inputs are finite; a program needn't handle non-finite values.
Results may differ from a plain program's by a relative error of at most 0.00829362.
Values are sent between devices in bfloat16 or wider.
A program may use at most 1 GiB of HBM per device.

v0:
```python
import jax
import jax.numpy as jnp
from jax import lax
from jax.sharding import PartitionSpec as P


def solution(mesh):
    row_len = mesh.shape['row']
    col_len = mesh.shape['col']

    def add_halo(act_tile, axis_name, edge_dim, axis_len):
        if edge_dim == 1:
            head_edge = act_tile[:, :1]
            tail_edge = act_tile[:, -1:]
        else:
            head_edge = act_tile[:, :, :1]
            tail_edge = act_tile[:, :, -1:]
        if axis_len == 1:
            from_prev = jnp.zeros_like(tail_edge)
            from_next = jnp.zeros_like(head_edge)
        else:
            to_next = [(i, i + 1) for i in range(axis_len - 1)]
            to_prev = [(i + 1, i) for i in range(axis_len - 1)]
            from_prev = lax.ppermute(tail_edge, axis_name, to_next)
            from_next = lax.ppermute(head_edge, axis_name, to_prev)
        return jnp.concatenate([from_prev, act_tile, from_next], axis=edge_dim)

    def conv_relu(act_tile, weight, bias_vec, stride):
        padded = add_halo(add_halo(act_tile, 'row', 1, row_len), 'col', 2, col_len)
        summed = lax.conv_general_dilated(padded, weight, (stride, stride), 'VALID', dimension_numbers=('NHWC', 'HWIO', 'NHWC'), preferred_element_type=jnp.float32)
        return jax.nn.relu(summed + bias_vec).astype(jnp.bfloat16)

    def local_encoder(images, w_down1, b_down1, w_conv1, b_conv1, w_down2, b_down2, w_conv2, b_conv2, w_down3, b_down3, w_conv3, b_conv3):
        params = [(w_down1, b_down1, w_conv1, b_conv1), (w_down2, b_down2, w_conv2, b_conv2), (w_down3, b_down3, w_conv3, b_conv3)]
        act_tile = images
        for w_down, b_down, w_conv, b_conv in params:
            act_tile = conv_relu(act_tile, w_down, b_down, 2)
            act_tile = conv_relu(act_tile, w_conv, b_conv, 1)
        return act_tile

    tile_spec = P('batch', 'row', 'col', None)
    return jax.shard_map(local_encoder, mesh=mesh, in_specs=(tile_spec,) + (P(),) * 12, out_specs=tile_spec, check_vma=False)
```

profile of v0, /device:TPU:97, one launch (start us, length us, event | category | flops | bytes accessed | tf_op | source)
XLA Modules:
  0.0 135.2 jit_solution(15851203994422027980)
XLA Ops:
  0.0 1.2 fusion.79
  1.4 3.1 %collective-permute-start = (bf16[16,1,64,128]{3,0,2,1:T(8,128)(2,1)S(1)}, bf16[16,1,64,128]{3,0,2,1:T(8,128)(2,1)S(1)}, u32[]{:S(2)}, u32[]{:S(2)}) collective-permute-start(bf16[16,1,64,128]{3,0,2,1:T(8,128)(2,1)S(1)} %copy.19), channel_id=1, source_target_pairs={{0,1},{1,2},{2,3},{3,4},{4,5},{5,6},{6,7},{7,8},{8,9},{9,10},{10,1... | collective-permute-start | bytes 786440 | tf_op jit(solution)/shard_map/ppermute | solution.py:24
  4.7 6.4 %collective-permute-start.1 = (bf16[16,1,64,128]{3,0,2,1:T(8,128)(2,1)S(1)}, bf16[16,1,64,128]{3,0,2,1:T(8,128)(2,1)S(1)}, u32[]{:S(2)}, u32[]{:S(2)}) collective-permute-start(bf16[16,1,64,128]{3,0,2,1:T(8,128)(2,1)S(1)} %copy.20), channel_id=1, source_target_pairs={{1,0},{2,1},{3,2},{4,3},{5,4},{6,5},{7,6},{8,7},{9,8},{10,9},{11,1... | collective-permute-start | bytes 786440 | tf_op jit(solution)/shard_map/ppermute | solution.py:25
  11.1 3.6 %collective-permute-done = bf16[16,1,64,128]{3,0,2,1:T(8,128)(2,1)S(1)} collective-permute-done((bf16[16,1,64,128]{3,0,2,1:T(8,128)(2,1)S(1)}, bf16[16,1,64,128]{3,0,2,1:T(8,128)(2,1)S(1)}, u32[]{:S(2)}, u32[]{:S(2)}) %collective-permute-start) | collective-permute-done | bytes 262176 | tf_op jit(solution)/shard_map/ppermute | solution.py:24
  14.8 1.6 %constant_dynamic-update-slice_fusion.1 = bf16[16,10,64,128]{3,0,2,1:T(8,128)(2,1)S(1)} fusion(bf16[16,10,64,128]{3,0,2,1:T(8,128)(2,1)S(1)} %constant_dynamic-update-slice_fusion.2, bf16[16,8,64,128]{3,2,1,0:T(8,128)(2,1)S(1)} %copy-done.1), kind=kLoop, calls=%fused_computation.83 | loop fusion | bytes 4194304
  16.4 1.3 collective-permute-start.2
  17.7 4.0 %collective-permute-start.3 = (bf16[16,10,1,128]{3,0,2,1:T(8,128)(2,1)S(1)}, bf16[16,10,1,128]{3,0,2,1:T(8,128)(2,1)S(1)}, u32[]{:S(2)}, u32[]{:S(2)}) collective-permute-start(bf16[16,10,1,128]{3,0,2,1:T(8,128)(2,1)S(1)} %get-tuple-element.6), channel_id=1, source_target_pairs={{64,0},{65,1},{66,2},{67,3},{68,4},{69,5},{70,6},{71,7},{72,8},{73... | collective-permute-start | bytes 122888 | tf_op jit(solution)/shard_map/ppermute | solution.py:25
  21.7 0.8 collective-permute-done.3
  22.6 2.4 %maximum_convert_fusion.1 = bf16[16,4,32,256]{3,0,2,1:T(8,128)(2,1)S(1)} fusion(bf16[4,4,128,256]{3,2,1,0:T(8,128)(2,1)S(1)} %copy-done.6, bf16[16,10,1,128]{3,0,2,1:T(8,128)(2,1)S(1)} %collective-permute-done.3, bf16[16,10,64,128]{3,0,2,1:T(8,128)(2,1)S(1)} %constant_dynamic-update-slice_fusion, bf16[16,10,1,128]{3,0,2,1:T(8,128)(2,1)S(1)} %collective-permute-done.2, ...), kind=kOutput, calls=%fused_computation.7 | convolution fusion | flops 2151759872 | bytes 4801536 | tf_op jit(solution)/shard_map/conv_general_dilated | solution.py:30
  25.0 2.1 %collective-permute-start.4 = (bf16[16,1,32,256]{3,0,2,1:T(8,128)(2,1)S(1)}, bf16[16,1,32,256]{3,0,2,1:T(8,128)(2,1)S(1)}, u32[]{:S(2)}, u32[]{:S(2)}) collective-permute-start(bf16[16,1,32,256]{3,0,2,1:T(8,128)(2,1)S(1)} %get-tuple-element.15), channel_id=1, source_target_pairs={{0,1},{1,2},{2,3},{3,4},{4,5},{5,6},{6,7},{7,8},{8,9},{9,10},{10,1... | collective-permute-start | bytes 786440 | tf_op jit(solution)/shard_map/ppermute | solution.py:24
  27.1 8.1 %collective-permute-start.5 = (bf16[16,1,32,256]{3,0,2,1:T(8,128)(2,1)S(1)}, bf16[16,1,32,256]{3,0,2,1:T(8,128)(2,1)S(1)}, u32[]{:S(2)}, u32[]{:S(2)}) collective-permute-start(bf16[16,1,32,256]{3,0,2,1:T(8,128)(2,1)S(1)} %get-tuple-element.16), channel_id=1, source_target_pairs={{1,0},{2,1},{3,2},{4,3},{5,4},{6,5},{7,6},{8,7},{9,8},{10,9},{11,1... | collective-permute-start | bytes 786440 | tf_op jit(solution)/shard_map/ppermute | solution.py:25
  35.2 4.4 %collective-permute-done.4 = bf16[16,1,32,256]{3,0,2,1:T(8,128)(2,1)S(1)} collective-permute-done((bf16[16,1,32,256]{3,0,2,1:T(8,128)(2,1)S(1)}, bf16[16,1,32,256]{3,0,2,1:T(8,128)(2,1)S(1)}, u32[]{:S(2)}, u32[]{:S(2)}) %collective-permute-start.4) | collective-permute-done | bytes 262176 | tf_op jit(solution)/shard_map/ppermute | solution.py:24
  39.6 0.9 collective-permute-done.5
  40.5 1.3 collective-permute-start.6
  41.8 3.6 %collective-permute-start.7 = (bf16[16,6,1,256]{3,0,2,1:T(8,128)(2,1)S(1)}, bf16[16,6,1,256]{3,0,2,1:T(8,128)(2,1)S(1)}, u32[]{:S(2)}, u32[]{:S(2)}) collective-permute-start(bf16[16,6,1,256]{3,0,2,1:T(8,128)(2,1)S(1)} %get-tuple-element.12), channel_id=1, source_target_pairs={{64,0},{65,1},{66,2},{67,3},{68,4},{69,5},{70,6},{71,7},{72,8},{73... | collective-permute-start | bytes 147464 | tf_op jit(solution)/shard_map/ppermute | solution.py:25
  45.4 0.9 collective-permute-done.7
  46.3 2.7 %maximum_convert_fusion = bf16[16,4,32,256]{3,0,2,1:T(8,128)(2,1)S(1)} fusion(bf16[3,3,256,256]{3,2,1,0:T(8,128)(2,1)S(1)} %copy-done.3, bf16[16,6,1,256]{3,0,2,1:T(8,128)(2,1)S(1)} %collective-permute-done.7, bf16[16,1,32,256]{3,0,2,1:T(8,128)(2,1)S(1)} %collective-permute-done.5, bf16[16,4,32,256]{3,0,2,1:T(8,128)(2,1)S(1)} %maximum_convert_fusion.1, ...), kind=kOutput, calls=%fused_computation.6 | convolution fusion | flops 2420834304 | bytes 3900416 | tf_op jit(solution)/shard_map/conv_general_dilated | solution.py:30
  49.0 1.9 %collective-permute-start.8 = (bf16[16,1,32,256]{3,0,2,1:T(8,128)(2,1)S(1)}, bf16[16,1,32,256]{3,0,2,1:T(8,128)(2,1)S(1)}, u32[]{:S(2)}, u32[]{:S(2)}) collective-permute-start(bf16[16,1,32,256]{3,0,2,1:T(8,128)(2,1)S(1)} %get-tuple-element.13), channel_id=1, source_target_pairs={{0,1},{1,2},{2,3},{3,4},{4,5},{5,6},{6,7},{7,8},{8,9},{9,10},{10,1... | collective-permute-start | bytes 786440 | tf_op jit(solution)/shard_map/ppermute | solution.py:24
  50.9 8.4 %collective-permute-start.9 = (bf16[16,1,32,256]{3,0,2,1:T(8,128)(2,1)S(1)}, bf16[16,1,32,256]{3,0,2,1:T(8,128)(2,1)S(1)}, u32[]{:S(2)}, u32[]{:S(2)}) collective-permute-start(bf16[16,1,32,256]{3,0,2,1:T(8,128)(2,1)S(1)} %get-tuple-element.14), channel_id=1, source_target_pairs={{1,0},{2,1},{3,2},{4,3},{5,4},{6,5},{7,6},{8,7},{9,8},{10,9},{11,1... | collective-permute-start | bytes 786440 | tf_op jit(solution)/shard_map/ppermute | solution.py:25
  59.3 4.4 %collective-permute-done.8 = bf16[16,1,32,256]{3,0,2,1:T(8,128)(2,1)S(1)} collective-permute-done((bf16[16,1,32,256]{3,0,2,1:T(8,128)(2,1)S(1)}, bf16[16,1,32,256]{3,0,2,1:T(8,128)(2,1)S(1)}, u32[]{:S(2)}, u32[]{:S(2)}) %collective-permute-start.8) | collective-permute-done | bytes 262176 | tf_op jit(solution)/shard_map/ppermute | solution.py:24
  63.7 0.9 collective-permute-done.9
  64.6 1.3 collective-permute-start.10
  65.9 3.8 %collective-permute-start.11 = (bf16[16,6,1,256]{3,0,2,1:T(8,128)(2,1)S(1)}, bf16[16,6,1,256]{3,0,2,1:T(8,128)(2,1)S(1)}, u32[]{:S(2)}, u32[]{:S(2)}) collective-permute-start(bf16[16,6,1,256]{3,0,2,1:T(8,128)(2,1)S(1)} %get-tuple-element.10), channel_id=1, source_target_pairs={{64,0},{65,1},{66,2},{67,3},{68,4},{69,5},{70,6},{71,7},{72,8},{73... | collective-permute-start | bytes 147464 | tf_op jit(solution)/shard_map/ppermute | solution.py:25
  69.7 0.9 collective-permute-done.11
  70.5 1.3 fusion.37
  71.8 1.9 %collective-permute-start.12 = (bf16[16,1,16,256]{3,0,2,1:T(8,128)(2,1)S(1)}, bf16[16,1,16,256]{3,0,2,1:T(8,128)(2,1)S(1)}, u32[]{:S(2)}, u32[]{:S(2)}) collective-permute-start(bf16[16,1,16,256]{3,0,2,1:T(8,128)(2,1)S(1)} %get-tuple-element.23), channel_id=1, source_target_pairs={{0,1},{1,2},{2,3},{3,4},{4,5},{5,6},{6,7},{7,8},{8,9},{9,10},{10,1... | collective-permute-start | bytes 393224 | tf_op jit(solution)/shard_map/ppermute | solution.py:24
  73.8 8.3 %collective-permute-start.13 = (bf16[16,1,16,256]{3,0,2,1:T(8,128)(2,1)S(1)}, bf16[16,1,16,256]{3,0,2,1:T(8,128)(2,1)S(1)}, u32[]{:S(2)}, u32[]{:S(2)}) collective-permute-start(bf16[16,1,16,256]{3,0,2,1:T(8,128)(2,1)S(1)} %get-tuple-element.24), channel_id=1, source_target_pairs={{1,0},{2,1},{3,2},{4,3},{5,4},{6,5},{7,6},{8,7},{9,8},{10,9},{11,1... | collective-permute-start | bytes 393224 | tf_op jit(solution)/shard_map/ppermute | solution.py:25
  82.1 1.6 %collective-permute-done.12 = bf16[16,1,16,256]{3,0,2,1:T(8,128)(2,1)S(1)} collective-permute-done((bf16[16,1,16,256]{3,0,2,1:T(8,128)(2,1)S(1)}, bf16[16,1,16,256]{3,0,2,1:T(8,128)(2,1)S(1)}, u32[]{:S(2)}, u32[]{:S(2)}) %collective-permute-start.12) | collective-permute-done | bytes 131104 | tf_op jit(solution)/shard_map/ppermute | solution.py:24
  83.7 0.9 collective-permute-done.13
  84.6 1.3 collective-permute-start.14
  85.9 3.9 %collective-permute-start.15 = (bf16[16,4,1,256]{3,0,2,1:T(8,128)(2,1)S(1)}, bf16[16,4,1,256]{3,0,2,1:T(8,128)(2,1)S(1)}, u32[]{:S(2)}, u32[]{:S(2)}) collective-permute-start(bf16[16,4,1,256]{3,0,2,1:T(8,128)(2,1)S(1)} %get-tuple-element.20), channel_id=1, source_target_pairs={{64,0},{65,1},{66,2},{67,3},{68,4},{69,5},{70,6},{71,7},{72,8},{73... | collective-permute-start | bytes 98312 | tf_op jit(solution)/shard_map/ppermute | solution.py:25
  89.8 0.8 collective-permute-done.15
  90.7 0.8 fusion.40
  91.5 1.9 %collective-permute-start.16 = (bf16[16,1,16,256]{3,0,2,1:T(8,128)(2,1)S(1)}, bf16[16,1,16,256]{3,0,2,1:T(8,128)(2,1)S(1)}, u32[]{:S(2)}, u32[]{:S(2)}) collective-permute-start(bf16[16,1,16,256]{3,0,2,1:T(8,128)(2,1)S(1)} %get-tuple-element.21), channel_id=1, source_target_pairs={{0,1},{1,2},{2,3},{3,4},{4,5},{5,6},{6,7},{7,8},{8,9},{9,10},{10,1... | collective-permute-start | bytes 393224 | tf_op jit(solution)/shard_map/ppermute | solution.py:24
  93.4 8.3 %collective-permute-start.17 = (bf16[16,1,16,256]{3,0,2,1:T(8,128)(2,1)S(1)}, bf16[16,1,16,256]{3,0,2,1:T(8,128)(2,1)S(1)}, u32[]{:S(2)}, u32[]{:S(2)}) collective-permute-start(bf16[16,1,16,256]{3,0,2,1:T(8,128)(2,1)S(1)} %get-tuple-element.22), channel_id=1, source_target_pairs={{1,0},{2,1},{3,2},{4,3},{5,4},{6,5},{7,6},{8,7},{9,8},{10,9},{11,1... | collective-permute-start | bytes 393224 | tf_op jit(solution)/shard_map/ppermute | solution.py:25
  101.8 1.6 %collective-permute-done.16 = bf16[16,1,16,256]{3,0,2,1:T(8,128)(2,1)S(1)} collective-permute-done((bf16[16,1,16,256]{3,0,2,1:T(8,128)(2,1)S(1)}, bf16[16,1,16,256]{3,0,2,1:T(8,128)(2,1)S(1)}, u32[]{:S(2)}, u32[]{:S(2)}) %collective-permute-start.16) | collective-permute-done | bytes 131104 | tf_op jit(solution)/shard_map/ppermute | solution.py:24
  103.3 0.9 collective-permute-done.17
  104.2 1.3 collective-permute-start.18
  105.6 3.9 %collective-permute-start.19 = (bf16[16,4,1,256]{3,0,2,1:T(8,128)(2,1)S(1)}, bf16[16,4,1,256]{3,0,2,1:T(8,128)(2,1)S(1)}, u32[]{:S(2)}, u32[]{:S(2)}) collective-permute-start(bf16[16,4,1,256]{3,0,2,1:T(8,128)(2,1)S(1)} %get-tuple-element.18), channel_id=1, source_target_pairs={{64,0},{65,1},{66,2},{67,3},{68,4},{69,5},{70,6},{71,7},{72,8},{73... | collective-permute-start | bytes 98312 | tf_op jit(solution)/shard_map/ppermute | solution.py:25
  109.5 0.8 collective-permute-done.19
  110.3 0.5 fusion.44
  110.8 8.3 %collective-permute-start.21 = (bf16[16,1,8,256]{3,0,2,1:T(8,128)(2,1)S(1)}, bf16[16,1,8,256]{3,0,2,1:T(8,128)(2,1)S(1)}, u32[]{:S(2)}, u32[]{:S(2)}) collective-permute-start(bf16[16,1,8,256]{3,0,2,1:T(8,128)(2,1)S(1)} %fusion.44), channel_id=1, source_target_pairs={{1,0},{2,1},{3,2},{4,3},{5,4},{6,5},{7,6},{8,7},{9,8},{10,9},{11,1... | collective-permute-start | bytes 196616 | tf_op jit(solution)/shard_map/ppermute | solution.py:25
  119.1 1.9 %collective-permute-start.20 = (bf16[16,1,8,256]{3,0,2,1:T(8,128)(2,1)S(1)}, bf16[16,1,8,256]{3,0,2,1:T(8,128)(2,1)S(1)}, u32[]{:S(2)}, u32[]{:S(2)}) collective-permute-start(bf16[16,1,8,256]{3,0,2,1:T(8,128)(2,1)S(1)} %fusion.44), channel_id=1, source_target_pairs={{0,1},{1,2},{2,3},{3,4},{4,5},{5,6},{6,7},{7,8},{8,9},{9,10},{10,1... | collective-permute-start | bytes 196616 | tf_op jit(solution)/shard_map/ppermute | solution.py:24
  121.0 7.3 %collective-permute-done.20 = bf16[16,1,8,256]{3,0,2,1:T(8,128)(2,1)S(1)} collective-permute-done((bf16[16,1,8,256]{3,0,2,1:T(8,128)(2,1)S(1)}, bf16[16,1,8,256]{3,0,2,1:T(8,128)(2,1)S(1)}, u32[]{:S(2)}, u32[]{:S(2)}) %collective-permute-start.20) | collective-permute-done | bytes 65568 | tf_op jit(solution)/shard_map/ppermute | solution.py:24
  128.3 1.3 collective-permute-start.22
  129.6 3.7 %collective-permute-start.23 = (bf16[16,3,1,256]{3,0,2,1:T(8,128)(2,1)S(1)}, bf16[16,3,1,256]{3,0,2,1:T(8,128)(2,1)S(1)}, u32[]{:S(2)}, u32[]{:S(2)}) collective-permute-start(bf16[16,3,1,256]{3,0,2,1:T(8,128)(2,1)S(1)} %get-tuple-element.26), channel_id=1, source_target_pairs={{64,0},{65,1},{66,2},{67,3},{68,4},{69,5},{70,6},{71,7},{72,8},{73... | collective-permute-start | bytes 73736 | tf_op jit(solution)/shard_map/ppermute | solution.py:25
  133.3 0.8 collective-permute-done.23
  134.5 0.7 copy.17
  (49 shorter events, 1.0 us)
Async XLA Ops:
  0.0 70.5 %copy-start = (bf16[4,4,256,256]{3,2,1,0:T(8,128)(2,1)S(1)}, bf16[4,4,256,256]{3,2,1,0:T(8,128)(2,1)}, u32[]{:S(2)}) copy-start(bf16[4,4,256,256]{3,2,1,0:T(8,128)(2,1)} %param.18) | copy-start | bytes 6291460
  0.0 14.7 %copy-start.1 = (bf16[16,8,64,128]{3,2,1,0:T(8,128)(2,1)S(1)}, bf16[16,8,64,128]{3,2,1,0:T(8,128)(2,1)}, u32[]{:S(2)}) copy-start(bf16[16,8,64,128]{3,2,1,0:T(8,128)(2,1)} %param.13) | copy-start | bytes 6291460
  1.4 13.3 %collective-permute-start = (bf16[16,1,64,128]{3,0,2,1:T(8,128)(2,1)S(1)}, bf16[16,1,64,128]{3,0,2,1:T(8,128)(2,1)S(1)}, u32[]{:S(2)}, u32[]{:S(2)}) collective-permute-start(bf16[16,1,64,128]{3,0,2,1:T(8,128)(2,1)S(1)} %copy.19), channel_id=1, source_target_pairs={{0,1},{1,2},{2,3},{3,4},{4,5},{5,6},{6,7},{7,8},{8,9},{9,10},{10,1... | collective-permute-start | bytes 786440 | tf_op jit(solution)/shard_map/ppermute | solution.py:24
  4.7 11.6 %collective-permute-start.1 = (bf16[16,1,64,128]{3,0,2,1:T(8,128)(2,1)S(1)}, bf16[16,1,64,128]{3,0,2,1:T(8,128)(2,1)S(1)}, u32[]{:S(2)}, u32[]{:S(2)}) collective-permute-start(bf16[16,1,64,128]{3,0,2,1:T(8,128)(2,1)S(1)} %copy.20), channel_id=1, source_target_pairs={{1,0},{2,1},{3,2},{4,3},{5,4},{6,5},{7,6},{8,7},{9,8},{10,9},{11,1... | collective-permute-start | bytes 786440 | tf_op jit(solution)/shard_map/ppermute | solution.py:25
  14.7 7.8 %copy-start.6 = (bf16[4,4,128,256]{3,2,1,0:T(8,128)(2,1)S(1)}, bf16[4,4,128,256]{3,2,1,0:T(8,128)(2,1)}, u32[]{:S(2)}) copy-start(bf16[4,4,128,256]{3,2,1,0:T(8,128)(2,1)} %param.14) | copy-start | bytes 3145732
  14.8 7.8 %copy-start.7 = (f32[256]{0:T(256)S(1)}, f32[256]{0:T(256)}, u32[]{:S(2)}) copy-start(f32[256]{0:T(256)} %param.15) | copy-start | bytes 3076
  16.4 5.3 %collective-permute-start.2 = (bf16[16,10,1,128]{3,0,2,1:T(8,128)(2,1)S(1)}, bf16[16,10,1,128]{3,0,2,1:T(8,128)(2,1)S(1)}, u32[]{:S(2)}, u32[]{:S(2)}) collective-permute-start(bf16[16,10,1,128]{3,0,2,1:T(8,128)(2,1)S(1)} %get-tuple-element.5), channel_id=1, source_target_pairs={{0,64},{1,65},{2,66},{3,67},{4,68},{5,69},{6,70},{7,71},{8,72},{9,... | collective-permute-start | bytes 122888 | tf_op jit(solution)/shard_map/ppermute | solution.py:24
  17.7 4.9 %collective-permute-start.3 = (bf16[16,10,1,128]{3,0,2,1:T(8,128)(2,1)S(1)}, bf16[16,10,1,128]{3,0,2,1:T(8,128)(2,1)S(1)}, u32[]{:S(2)}, u32[]{:S(2)}) collective-permute-start(bf16[16,10,1,128]{3,0,2,1:T(8,128)(2,1)S(1)} %get-tuple-element.6), channel_id=1, source_target_pairs={{64,0},{65,1},{66,2},{67,3},{68,4},{69,5},{70,6},{71,7},{72,8},{73... | collective-permute-start | bytes 122888 | tf_op jit(solution)/shard_map/ppermute | solution.py:25
  24.9 21.3 %copy-start.3 = (bf16[3,3,256,256]{3,2,1,0:T(8,128)(2,1)S(1)}, bf16[3,3,256,256]{3,2,1,0:T(8,128)(2,1)}, u32[]{:S(2)}) copy-start(bf16[3,3,256,256]{3,2,1,0:T(8,128)(2,1)} %param.16) | copy-start | bytes 3538948
  25.0 21.3 %copy-start.8 = (f32[256]{0:T(256)S(1)}, f32[256]{0:T(256)}, u32[]{:S(2)}) copy-start(f32[256]{0:T(256)} %param.17) | copy-start | bytes 3076
  25.0 14.5 %collective-permute-start.4 = (bf16[16,1,32,256]{3,0,2,1:T(8,128)(2,1)S(1)}, bf16[16,1,32,256]{3,0,2,1:T(8,128)(2,1)S(1)}, u32[]{:S(2)}, u32[]{:S(2)}) collective-permute-start(bf16[16,1,32,256]{3,0,2,1:T(8,128)(2,1)S(1)} %get-tuple-element.15), channel_id=1, source_target_pairs={{0,1},{1,2},{2,3},{3,4},{4,5},{5,6},{6,7},{7,8},{8,9},{9,10},{10,1... | collective-permute-start | bytes 786440 | tf_op jit(solution)/shard_map/ppermute | solution.py:24
  27.1 13.4 %collective-permute-start.5 = (bf16[16,1,32,256]{3,0,2,1:T(8,128)(2,1)S(1)}, bf16[16,1,32,256]{3,0,2,1:T(8,128)(2,1)S(1)}, u32[]{:S(2)}, u32[]{:S(2)}) collective-permute-start(bf16[16,1,32,256]{3,0,2,1:T(8,128)(2,1)S(1)} %get-tuple-element.16), channel_id=1, source_target_pairs={{1,0},{2,1},{3,2},{4,3},{5,4},{6,5},{7,6},{8,7},{9,8},{10,9},{11,1... | collective-permute-start | bytes 786440 | tf_op jit(solution)/shard_map/ppermute | solution.py:25
  40.5 4.9 %collective-permute-start.6 = (bf16[16,6,1,256]{3,0,2,1:T(8,128)(2,1)S(1)}, bf16[16,6,1,256]{3,0,2,1:T(8,128)(2,1)S(1)}, u32[]{:S(2)}, u32[]{:S(2)}) collective-permute-start(bf16[16,6,1,256]{3,0,2,1:T(8,128)(2,1)S(1)} %get-tuple-element.11), channel_id=1, source_target_pairs={{0,64},{1,65},{2,66},{3,67},{4,68},{5,69},{6,70},{7,71},{8,72},{9,... | collective-permute-start | bytes 147464 | tf_op jit(solution)/shard_map/ppermute | solution.py:24
  41.8 4.5 %collective-permute-start.7 = (bf16[16,6,1,256]{3,0,2,1:T(8,128)(2,1)S(1)}, bf16[16,6,1,256]{3,0,2,1:T(8,128)(2,1)S(1)}, u32[]{:S(2)}, u32[]{:S(2)}) collective-permute-start(bf16[16,6,1,256]{3,0,2,1:T(8,128)(2,1)S(1)} %get-tuple-element.12), channel_id=1, source_target_pairs={{64,0},{65,1},{66,2},{67,3},{68,4},{69,5},{70,6},{71,7},{72,8},{73... | collective-permute-start | bytes 147464 | tf_op jit(solution)/shard_map/ppermute | solution.py:25
  48.9 21.6 %copy-start.9 = (f32[256]{0:T(256)S(1)}, f32[256]{0:T(256)}, u32[]{:S(2)}) copy-start(f32[256]{0:T(256)} %param.19) | copy-start | bytes 3076
  49.0 14.7 %collective-permute-start.8 = (bf16[16,1,32,256]{3,0,2,1:T(8,128)(2,1)S(1)}, bf16[16,1,32,256]{3,0,2,1:T(8,128)(2,1)S(1)}, u32[]{:S(2)}, u32[]{:S(2)}) collective-permute-start(bf16[16,1,32,256]{3,0,2,1:T(8,128)(2,1)S(1)} %get-tuple-element.13), channel_id=1, source_target_pairs={{0,1},{1,2},{2,3},{3,4},{4,5},{5,6},{6,7},{7,8},{8,9},{9,10},{10,1... | collective-permute-start | bytes 786440 | tf_op jit(solution)/shard_map/ppermute | solution.py:24
  50.9 13.6 %collective-permute-start.9 = (bf16[16,1,32,256]{3,0,2,1:T(8,128)(2,1)S(1)}, bf16[16,1,32,256]{3,0,2,1:T(8,128)(2,1)S(1)}, u32[]{:S(2)}, u32[]{:S(2)}) collective-permute-start(bf16[16,1,32,256]{3,0,2,1:T(8,128)(2,1)S(1)} %get-tuple-element.14), channel_id=1, source_target_pairs={{1,0},{2,1},{3,2},{4,3},{5,4},{6,5},{7,6},{8,7},{9,8},{10,9},{11,1... | collective-permute-start | bytes 786440 | tf_op jit(solution)/shard_map/ppermute | solution.py:25
  64.6 5.1 %collective-permute-start.10 = (bf16[16,6,1,256]{3,0,2,1:T(8,128)(2,1)S(1)}, bf16[16,6,1,256]{3,0,2,1:T(8,128)(2,1)S(1)}, u32[]{:S(2)}, u32[]{:S(2)}) collective-permute-start(bf16[16,6,1,256]{3,0,2,1:T(8,128)(2,1)S(1)} %get-tuple-element.9), channel_id=1, source_target_pairs={{0,64},{1,65},{2,66},{3,67},{4,68},{5,69},{6,70},{7,71},{8,72},{9,... | collective-permute-start | bytes 147464 | tf_op jit(solution)/shard_map/ppermute | solution.py:24
  65.9 24.8 %copy-start.4 = (bf16[3,3,256,256]{3,2,1,0:T(8,128)(2,1)S(1)}, bf16[3,3,256,256]{3,2,1,0:T(8,128)(2,1)}, u32[]{:S(2)}) copy-start(bf16[3,3,256,256]{3,2,1,0:T(8,128)(2,1)} %param.20) | copy-start | bytes 3538948
  65.9 24.8 %copy-start.10 = (f32[256]{0:T(256)S(1)}, f32[256]{0:T(256)}, u32[]{:S(2)}) copy-start(f32[256]{0:T(256)} %param.21) | copy-start | bytes 3076
  65.9 4.6 %collective-permute-start.11 = (bf16[16,6,1,256]{3,0,2,1:T(8,128)(2,1)S(1)}, bf16[16,6,1,256]{3,0,2,1:T(8,128)(2,1)S(1)}, u32[]{:S(2)}, u32[]{:S(2)}) collective-permute-start(bf16[16,6,1,256]{3,0,2,1:T(8,128)(2,1)S(1)} %get-tuple-element.10), channel_id=1, source_target_pairs={{64,0},{65,1},{66,2},{67,3},{68,4},{69,5},{70,6},{71,7},{72,8},{73... | collective-permute-start | bytes 147464 | tf_op jit(solution)/shard_map/ppermute | solution.py:25
  71.8 11.9 %collective-permute-start.12 = (bf16[16,1,16,256]{3,0,2,1:T(8,128)(2,1)S(1)}, bf16[16,1,16,256]{3,0,2,1:T(8,128)(2,1)S(1)}, u32[]{:S(2)}, u32[]{:S(2)}) collective-permute-start(bf16[16,1,16,256]{3,0,2,1:T(8,128)(2,1)S(1)} %get-tuple-element.23), channel_id=1, source_target_pairs={{0,1},{1,2},{2,3},{3,4},{4,5},{5,6},{6,7},{7,8},{8,9},{9,10},{10,1... | collective-permute-start | bytes 393224 | tf_op jit(solution)/shard_map/ppermute | solution.py:24
  73.8 10.8 %collective-permute-start.13 = (bf16[16,1,16,256]{3,0,2,1:T(8,128)(2,1)S(1)}, bf16[16,1,16,256]{3,0,2,1:T(8,128)(2,1)S(1)}, u32[]{:S(2)}, u32[]{:S(2)}) collective-permute-start(bf16[16,1,16,256]{3,0,2,1:T(8,128)(2,1)S(1)} %get-tuple-element.24), channel_id=1, source_target_pairs={{1,0},{2,1},{3,2},{4,3},{5,4},{6,5},{7,6},{8,7},{9,8},{10,9},{11,1... | collective-permute-start | bytes 393224 | tf_op jit(solution)/shard_map/ppermute | solution.py:25
  84.6 5.2 %collective-permute-start.14 = (bf16[16,4,1,256]{3,0,2,1:T(8,128)(2,1)S(1)}, bf16[16,4,1,256]{3,0,2,1:T(8,128)(2,1)S(1)}, u32[]{:S(2)}, u32[]{:S(2)}) collective-permute-start(bf16[16,4,1,256]{3,0,2,1:T(8,128)(2,1)S(1)} %get-tuple-element.19), channel_id=1, source_target_pairs={{0,64},{1,65},{2,66},{3,67},{4,68},{5,69},{6,70},{7,71},{8,72},{9,... | collective-permute-start | bytes 98312 | tf_op jit(solution)/shard_map/ppermute | solution.py:24
  85.9 24.4 %copy-start.2 = (bf16[4,4,256,256]{3,2,1,0:T(8,128)(2,1)S(1)}, bf16[4,4,256,256]{3,2,1,0:T(8,128)(2,1)}, u32[]{:S(2)}) copy-start(bf16[4,4,256,256]{3,2,1,0:T(8,128)(2,1)} %param.22) | copy-start | bytes 6291460
  85.9 24.4 %copy-start.11 = (f32[256]{0:T(256)S(1)}, f32[256]{0:T(256)}, u32[]{:S(2)}) copy-start(f32[256]{0:T(256)} %param.23) | copy-start | bytes 3076
  85.9 4.7 %collective-permute-start.15 = (bf16[16,4,1,256]{3,0,2,1:T(8,128)(2,1)S(1)}, bf16[16,4,1,256]{3,0,2,1:T(8,128)(2,1)S(1)}, u32[]{:S(2)}, u32[]{:S(2)}) collective-permute-start(bf16[16,4,1,256]{3,0,2,1:T(8,128)(2,1)S(1)} %get-tuple-element.20), channel_id=1, source_target_pairs={{64,0},{65,1},{66,2},{67,3},{68,4},{69,5},{70,6},{71,7},{72,8},{73... | collective-permute-start | bytes 98312 | tf_op jit(solution)/shard_map/ppermute | solution.py:25
  91.5 11.9 %collective-permute-start.16 = (bf16[16,1,16,256]{3,0,2,1:T(8,128)(2,1)S(1)}, bf16[16,1,16,256]{3,0,2,1:T(8,128)(2,1)S(1)}, u32[]{:S(2)}, u32[]{:S(2)}) collective-permute-start(bf16[16,1,16,256]{3,0,2,1:T(8,128)(2,1)S(1)} %get-tuple-element.21), channel_id=1, source_target_pairs={{0,1},{1,2},{2,3},{3,4},{4,5},{5,6},{6,7},{7,8},{8,9},{9,10},{10,1... | collective-permute-start | bytes 393224 | tf_op jit(solution)/shard_map/ppermute | solution.py:24
  93.4 10.8 %collective-permute-start.17 = (bf16[16,1,16,256]{3,0,2,1:T(8,128)(2,1)S(1)}, bf16[16,1,16,256]{3,0,2,1:T(8,128)(2,1)S(1)}, u32[]{:S(2)}, u32[]{:S(2)}) collective-permute-start(bf16[16,1,16,256]{3,0,2,1:T(8,128)(2,1)S(1)} %get-tuple-element.22), channel_id=1, source_target_pairs={{1,0},{2,1},{3,2},{4,3},{5,4},{6,5},{7,6},{8,7},{9,8},{10,9},{11,1... | collective-permute-start | bytes 393224 | tf_op jit(solution)/shard_map/ppermute | solution.py:25
  104.2 5.2 %collective-permute-start.18 = (bf16[16,4,1,256]{3,0,2,1:T(8,128)(2,1)S(1)}, bf16[16,4,1,256]{3,0,2,1:T(8,128)(2,1)S(1)}, u32[]{:S(2)}, u32[]{:S(2)}) collective-permute-start(bf16[16,4,1,256]{3,0,2,1:T(8,128)(2,1)S(1)} %get-tuple-element.17), channel_id=1, source_target_pairs={{0,64},{1,65},{2,66},{3,67},{4,68},{5,69},{6,70},{7,71},{8,72},{9,... | collective-permute-start | bytes 98312 | tf_op jit(solution)/shard_map/ppermute | solution.py:24
  105.5 28.6 %copy-start.5 = (bf16[3,3,256,256]{3,2,1,0:T(8,128)(2,1)S(1)}, bf16[3,3,256,256]{3,2,1,0:T(8,128)(2,1)}, u32[]{:S(2)}) copy-start(bf16[3,3,256,256]{3,2,1,0:T(8,128)(2,1)} %param.24) | copy-start | bytes 3538948
  105.6 28.6 %copy-start.12 = (f32[256]{0:T(256)S(1)}, f32[256]{0:T(256)}, u32[]{:S(2)}) copy-start(f32[256]{0:T(256)} %param.25) | copy-start | bytes 3076
  105.6 4.7 %collective-permute-start.19 = (bf16[16,4,1,256]{3,0,2,1:T(8,128)(2,1)S(1)}, bf16[16,4,1,256]{3,0,2,1:T(8,128)(2,1)S(1)}, u32[]{:S(2)}, u32[]{:S(2)}) collective-permute-start(bf16[16,4,1,256]{3,0,2,1:T(8,128)(2,1)S(1)} %get-tuple-element.18), channel_id=1, source_target_pairs={{64,0},{65,1},{66,2},{67,3},{68,4},{69,5},{70,6},{71,7},{72,8},{73... | collective-permute-start | bytes 98312 | tf_op jit(solution)/shard_map/ppermute | solution.py:25
  110.8 10.3 %collective-permute-start.21 = (bf16[16,1,8,256]{3,0,2,1:T(8,128)(2,1)S(1)}, bf16[16,1,8,256]{3,0,2,1:T(8,128)(2,1)S(1)}, u32[]{:S(2)}, u32[]{:S(2)}) collective-permute-start(bf16[16,1,8,256]{3,0,2,1:T(8,128)(2,1)S(1)} %fusion.44), channel_id=1, source_target_pairs={{1,0},{2,1},{3,2},{4,3},{5,4},{6,5},{7,6},{8,7},{9,8},{10,9},{11,1... | collective-permute-start | bytes 196616 | tf_op jit(solution)/shard_map/ppermute | solution.py:25
  119.1 9.2 %collective-permute-start.20 = (bf16[16,1,8,256]{3,0,2,1:T(8,128)(2,1)S(1)}, bf16[16,1,8,256]{3,0,2,1:T(8,128)(2,1)S(1)}, u32[]{:S(2)}, u32[]{:S(2)}) collective-permute-start(bf16[16,1,8,256]{3,0,2,1:T(8,128)(2,1)S(1)} %fusion.44), channel_id=1, source_target_pairs={{0,1},{1,2},{2,3},{3,4},{4,5},{5,6},{6,7},{7,8},{8,9},{9,10},{10,1... | collective-permute-start | bytes 196616 | tf_op jit(solution)/shard_map/ppermute | solution.py:24
  128.3 5.0 %collective-permute-start.22 = (bf16[16,3,1,256]{3,0,2,1:T(8,128)(2,1)S(1)}, bf16[16,3,1,256]{3,0,2,1:T(8,128)(2,1)S(1)}, u32[]{:S(2)}, u32[]{:S(2)}) collective-permute-start(bf16[16,3,1,256]{3,0,2,1:T(8,128)(2,1)S(1)} %get-tuple-element.25), channel_id=1, source_target_pairs={{0,64},{1,65},{2,66},{3,67},{4,68},{5,69},{6,70},{7,71},{8,72},{9,... | collective-permute-start | bytes 73736 | tf_op jit(solution)/shard_map/ppermute | solution.py:24
  129.6 4.5 %collective-permute-start.23 = (bf16[16,3,1,256]{3,0,2,1:T(8,128)(2,1)S(1)}, bf16[16,3,1,256]{3,0,2,1:T(8,128)(2,1)S(1)}, u32[]{:S(2)}, u32[]{:S(2)}) collective-permute-start(bf16[16,3,1,256]{3,0,2,1:T(8,128)(2,1)S(1)} %get-tuple-element.26), channel_id=1, source_target_pairs={{64,0},{65,1},{66,2},{67,3},{68,4},{69,5},{70,6},{71,7},{72,8},{73... | collective-permute-start | bytes 73736 | tf_op jit(solution)/shard_map/ppermute | solution.py:25
where the time goes:
time: 136 us; the launch traced here: 135 us
  starting transfers between devices  91.3 us (67%)
  waiting for transfers between devices  31.4 us (23%)
  matrix products  7.87 us (6%)
  local copies, waits for them, and re-layouts  4.04 us (3%)
    ppermute x12, starting transfers between devices, add_halo(): from_next = lax.ppermute(head_edge, axis_name, to_prev)  70.7 us
    ppermute x12, waiting for transfers between devices, add_halo(): from_prev = lax.ppermute(tail_edge, axis_name, to_next)  22.9 us
    ppermute x12, starting transfers between devices, add_halo(): from_prev = lax.ppermute(tail_edge, axis_name, to_next)  20.6 us
    ppermute x12, waiting for transfers between devices, add_halo(): from_next = lax.ppermute(head_edge, axis_name, to_prev)  8.55 us
    conv_general_dilated x6, matrix products, conv_relu(): lax.conv_general_dilated(padded, weight, (stride, stride), 'VALID', dimen...  7.87 us
  transfers between devices with their start and end apart: 24, of which 16 were waited for; matrix products, arithmetic and copies ran while one was open for 1% of the time, Pallas kernels for 0%

commit v1 on v0

v1 whole, which is shorter than its diff:
```python
import functools

import jax
import jax.numpy as jnp
from jax import lax
from jax.experimental import pallas as pl
from jax.experimental.pallas import tpu as pltpu
from jax.sharding import PartitionSpec as P

MESH = pl.DeviceIdType.MESH
LANES = 128
PAD = 8

GROUP = (2, 2, 4, 4, 8, 8)
CHUNK = (1, 1, 4, 4, 8, 8)


def plan(images, rows, width, c_in, c_out):
    layers = []
    for stage in range(3):
        for stride, taps in ((2, 4), (1, 3)):
            layers.append(
                dict(stride=stride, taps=taps, rows=rows, width=width, chan=c_in, out_rows=rows // stride, out_width=width // stride)
            )
            rows, width, c_in = rows // stride, width // stride, c_out
    for i, layer in enumerate(layers):
        layer["group"] = min(GROUP[i], images)
        layer["chunk"] = min(CHUNK[i], images)
        layer["groups"] = images // layer["group"]
    return layers


def kernel(layers, half, row_len, *refs):
    images_ref = refs[0]
    w_hbm, b_hbm = refs[1:13:2], refs[2:14:2]
    out_ref = refs[13]
    refs = refs[14:]
    ximg, xhalo, feat = refs[:3]
    w_refs, b_refs = refs[3:9], refs[9:15]
    a_refs = refs[15:21]
    s_refs = refs[21:27]
    send_bufs, halo_bufs = refs[27:32], refs[32:37]
    w_sem, b_sem, own_sem, part_send, part_recv, edge_send, edge_recv, out_sem = refs[37:45]
    y_send, y_recv = refs[45:50], refs[50:55]

    k = lax.axis_index("col")
    row = lax.axis_index("row")
    has = (row > 0, row < row_len - 1)
    near = (jnp.maximum(row - 1, 0), jnp.minimum(row + 1, row_len - 1))
    col_half = layers[0]["width"] // 2
    last_row = layers[0]["rows"] - 1

    barrier = pltpu.get_barrier_semaphore()
    pl.semaphore_signal(barrier, inc=1, device_id={"col": 1 - k}, device_id_type=MESH)
    for d in range(2):
        @pl.when(has[d])
        def _():
            for c in range(2):
                pl.semaphore_signal(barrier, inc=1, device_id={"col": c, "row": near[d]}, device_id_type=MESH)

    g0, n_groups0 = layers[0]["group"], layers[0]["groups"]

    def own_copy(g):
        src = images_ref.at[pl.ds(k * half + g * g0, g0)]
        return pltpu.make_async_copy(src, ximg.at[k, pl.ds(g * g0, g0)], own_sem.at[g])

    def part_copy(g):
        src = images_ref.at[pl.ds((1 - k) * half + g * g0, g0)]
        return pltpu.make_async_remote_copy(
            src, ximg.at[k, pl.ds(g * g0, g0)], part_send.at[g], part_recv.at[g], device_id={"col": 1 - k}, device_id_type=MESH
        )

    def part_arrival(g):
        dst = ximg.at[1 - k, pl.ds(g * g0, g0)]
        return pltpu.make_async_remote_copy(
            dst, dst, part_send.at[g], part_recv.at[g], device_id={"col": 1 - k}, device_id_type=MESH
        )

    def edge_copy(d, c, g):
        src = images_ref.at[pl.ds(c * half + g * g0, g0), 0 if d == 0 else last_row]
        return pltpu.make_async_remote_copy(
            src,
            xhalo.at[1 - d, k, pl.ds(g * g0, g0)],
            edge_send.at[d, c, g],
            edge_recv.at[1 - d, k, g],
            device_id={"col": c, "row": near[d]},
            device_id_type=MESH,
        )

    def edge_arrival(d, c, g):
        dst = xhalo.at[d, c, pl.ds(g * g0, g0)]
        return pltpu.make_async_remote_copy(
            dst, dst, edge_send.at[d, c, g], edge_recv.at[d, c, g], device_id={"col": c, "row": near[d]}, device_id_type=MESH
        )

    def y_copy(i, d, g):
        n = layers[i]["group"]
        return pltpu.make_async_remote_copy(
            send_bufs[i].at[d, pl.ds(g * n, n)],
            halo_bufs[i].at[1 - d, pl.ds(g * n, n)],
            y_send[i].at[d, g],
            y_recv[i].at[1 - d, g],
            device_id={"row": near[d]},
            device_id_type=MESH,
        )

    def y_arrival(i, d, g):
        n = layers[i]["group"]
        dst = halo_bufs[i].at[d, pl.ds(g * n, n)]
        return pltpu.make_async_remote_copy(
            dst, dst, y_send[i].at[d, g], y_recv[i].at[d, g], device_id={"row": near[d]}, device_id_type=MESH
        )

    def w_copy(i):
        return pltpu.make_async_copy(w_hbm[i], w_refs[i], w_sem.at[i])

    def b_copy(i):
        return pltpu.make_async_copy(b_hbm[i], b_refs[i], b_sem.at[i])

    own_copy(0).start()
    w_copy(0).start()
    for g in range(1, n_groups0):
        own_copy(g).start()
    for i in range(6):
        b_copy(i).start()
    for i in range(1, 6):
        w_copy(i).start()

    for i, layer in enumerate(layers):
        w = layer["width"]
        s = s_refs[i]
        edge = jnp.zeros(s.shape[:-2] + (PAD, LANES), jnp.float32)
        s[..., pl.ds(0, PAD), :] = edge
        s[..., pl.ds(PAD + w, PAD), :] = edge
    for d in range(2):
        @pl.when(jnp.logical_not(has[d]))
        def _():
            xhalo[d] = jnp.zeros(xhalo.shape[1:], xhalo.dtype)
            for h in halo_bufs:
                h[d] = jnp.zeros(h.shape[1:], h.dtype)

    pl.semaphore_wait(barrier, 1 + 2 * (has[0].astype(jnp.int32) + has[1].astype(jnp.int32)))

    for g in range(n_groups0):
        for d in range(2):
            @pl.when(has[d])
            def _():
                for c in range(2):
                    edge_copy(d, c, g).start()
        part_copy(g).start()

    def taps_from(i, slot, img, first, count):
        layer = layers[i]
        s, a = s_refs[i], a_refs[i]
        chan, w, stride = layer["chan"], layer["out_width"], layer["stride"]
        for q in range(layer["taps"]):
            for h in range(chan // LANES):
                lanes = pl.ds(q * chan + h * LANES, LANES)
                for r in range(first, first + count):
                    at = pl.ds(PAD - 1 + q, w) if stride == 1 else pl.ds(PAD - 1 + q, w, stride=2)
                    v = s[slot, h, r, at, :].astype(jnp.bfloat16)
                    if stride == 1:
                        a[img, r, :, lanes] = v
                    else:
                        a[img, r % 2, r // 2, :, lanes] = v

    def layer_step(i, g):
        layer = layers[i]
        n, chunk, rows, w = layer["group"], layer["chunk"], layer["rows"], layer["width"]
        out_rows, out_w, taps = layer["out_rows"], layer["out_width"], layer["taps"]
        s, a = s_refs[i], a_refs[i]
        base = g * n
        if i == 0:
            own_copy(g).wait()
            part_arrival(g).wait_recv()
            for d in range(2):
                @pl.when(has[d])
                def _():
                    for c in range(2):
                        edge_arrival(d, c, g).wait_recv()
        else:
            before = layers[i - 1]["group"]
            for d in range(2):
                @pl.when(has[d])
                def _():
                    for j in range(n // before):
                        y_arrival(i - 1, d, g * (n // before) + j).wait_recv()

        for m in range(0, n, chunk):
            imgs = [base + m + j for j in range(chunk)]
            for j, img in enumerate(imgs):
                slot = m + j
                if i == 0:
                    for c in range(2):
                        at = pl.ds(PAD + c * col_half, col_half)
                        s[slot, 0, 0, at, :] = xhalo[0, c, img].astype(jnp.float32)
                        s[slot, 0, pl.ds(1, rows), at, :] = ximg[c, img].astype(jnp.float32)
                        s[slot, 0, rows + 1, at, :] = xhalo[1, c, img].astype(jnp.float32)
                    taps_from(i, slot, slot, 0, rows + 2)
                else:
                    for d, r in ((0, 0), (1, rows + 1)):
                        v = halo_bufs[i - 1][d, img].astype(jnp.float32)
                        for h in range(layer["chan"] // LANES):
                            s[slot, h, r, pl.ds(PAD, w), :] = v[:, h * LANES : (h + 1) * LANES]
                        taps_from(i, slot, img, r, 1)
            size = chunk * out_rows * out_w
            first = m if i == 0 else base + m
            acc = None
            for p in range(taps):
                if layer["stride"] == 1:
                    left = a[pl.ds(first, chunk), pl.ds(p, out_rows)]
                else:
                    left = a[pl.ds(first, chunk), p % 2, pl.ds(p // 2, out_rows)]
                part = jnp.dot(left.reshape(size, left.shape[-1]), w_refs[i][p], preferred_element_type=jnp.float32)
                acc = part if acc is None else acc + part
            v = jnp.maximum(acc + b_refs[i][...], 0.0)
            c_out = v.shape[-1]
            if i == 5:
                v = v.reshape(chunk, out_w, c_out)
                for c in range(2):
                    feat[c, pl.ds(base + m, chunk)] = v[:, c * out_w // 2 : (c + 1) * out_w // 2].astype(jnp.bfloat16)
                continue
            v = v.reshape(chunk, out_rows, out_w, c_out)
            for d, r in ((0, 0), (1, out_rows - 1)):
                send_bufs[i][d, pl.ds(base + m, chunk)] = v[:, r].astype(jnp.bfloat16)
            nxt = s_refs[i + 1]
            slots = nxt.shape[0]
            for j, img in enumerate(imgs):
                slot = (m + j) % slots
                for h in range(c_out // LANES):
                    nxt[slot, h, pl.ds(1, out_rows), pl.ds(PAD, out_w), :] = v[j, :, :, h * LANES : (h + 1) * LANES]
                taps_from(i + 1, slot, img, 1, out_rows)
        if i < 5:
            for d in range(2):
                @pl.when(has[d])
                def _():
                    y_copy(i, d, g).start()

    for i in range(6):
        w_copy(i).wait()
        b_copy(i).wait()
        if layers[i]["groups"] == 1:
            layer_step(i, 0)
        else:
            @pl.loop(0, layers[i]["groups"])
            def _(g):
                layer_step(i, g)

    mine = pltpu.make_async_copy(feat.at[k], out_ref.at[pl.ds(k * half, half), 0], out_sem.at[0])
    theirs = pltpu.make_async_remote_copy(
        feat.at[1 - k],
        out_ref.at[pl.ds(k * half, half), 0],
        out_sem.at[1],
        out_sem.at[2],
        device_id={"col": 1 - k},
        device_id_type=MESH,
    )
    arriving = pltpu.make_async_remote_copy(
        feat.at[1 - k],
        out_ref.at[pl.ds((1 - k) * half, half), 0],
        out_sem.at[1],
        out_sem.at[2],
        device_id={"col": 1 - k},
        device_id_type=MESH,
    )
    theirs.start()
    mine.start()

    for g in range(n_groups0):
        part_copy(g).wait_send()
        for d in range(2):
            @pl.when(has[d])
            def _():
                for c in range(2):
                    edge_copy(d, c, g).wait_send()
    for i in range(5):
        for g in range(layers[i]["groups"]):
            for d in range(2):
                @pl.when(has[d])
                def _():
                    y_copy(i, d, g).wait_send()
    mine.wait()
    theirs.wait_send()
    arriving.wait_recv()


def solution(mesh):
    row_len = mesh.shape["row"]

    def local_encoder(images, *params):
        n_img, rows, col_half, c_in = images.shape
        half = n_img // 2
        weights, biases = params[0::2], params[1::2]
        c_out = weights[0].shape[-1]
        layers = plan(half, rows, 2 * col_half, c_in, c_out)
        args = [images]
        for w, b in zip(weights, biases):
            args += [w.reshape(w.shape[0], w.shape[1] * w.shape[2], c_out), b.reshape(1, c_out)]

        bf16, f32 = jnp.bfloat16, jnp.float32
        scratch = [
            pltpu.VMEM((2, half, rows, col_half, c_in), bf16),
            pltpu.VMEM((2, 2, half, col_half, c_in), bf16),
            pltpu.VMEM((2, half, layers[5]["out_width"] // 2, c_out), bf16),
        ]
        scratch += [pltpu.VMEM(w.shape, bf16) for w in args[1::2]]
        scratch += [pltpu.VMEM((1, c_out), f32) for _ in biases]
        for i, la in enumerate(layers):
            held = la["group"] if i == 0 else half
            depth = la["taps"] * la["chan"]
            if la["stride"] == 1:
                shape = (held, la["rows"] + 2, la["out_width"], depth)
            else:
                shape = (held, 2, (la["rows"] + 2) // 2, la["out_width"], depth)
            scratch.append(pltpu.VMEM(shape, bf16))
        for la in layers:
            scratch.append(pltpu.VMEM((la["group"], la["chan"] // LANES, la["rows"] + 2, la["width"] + 3 * PAD, LANES), f32))
        edges = [pltpu.VMEM((2, half, la["out_width"], c_out), bf16) for la in layers[:5]]
        scratch += edges + edges
        dma = pltpu.SemaphoreType.DMA
        g0 = layers[0]["groups"]
        scratch += [dma((6,)), dma((6,)), dma((g0,)), dma((g0,)), dma((g0,)), dma((2, 2, g0)), dma((2, 2, g0)), dma((3,))]
        sems = [dma((2, la["groups"])) for la in layers[:5]]
        scratch += sems + sems

        any_spec = pl.BlockSpec(memory_space=pl.ANY)
        return pl.pallas_call(
            functools.partial(kernel, layers, half, row_len),
            out_shape=jax.ShapeDtypeStruct((n_img, rows // 8, col_half // 8, c_out), bf16),
            in_specs=[any_spec] * len(args),
            out_specs=any_spec,
            scratch_shapes=scratch,
            compiler_params=pltpu.CompilerParams(collective_id=0, has_side_effects=True, vmem_limit_bytes=60 * 1024 * 1024),
            name="encoder",
        )(*args)

    tile_spec = P("batch", "row", "col", None)
    return jax.shard_map(local_encoder, mesh=mesh, in_specs=(tile_spec,) + (P(),) * 12, out_specs=tile_spec, check_vma=False)
```

time: 136 us -> 52 us (0.38)
  starting transfers between devices: 91.3 us -> 0 us
  Pallas kernels: 0 us -> 50.4 us
  waiting for transfers between devices: 31.4 us -> 0 us
  matrix products: 7.87 us -> 0 us
  local copies, waits for them, and re-layouts: 4.04 us -> 1.47 us
    ppermute x24 -> x0, starting transfers between devices: 91.3 us -> none  [the longest x12 70.7 us: add_halo(): from_next = lax.ppermute(head_edge, axis_name, to_prev)]
    pallas_call x0 -> x1, Pallas kernels: none -> 50.4 us  [local_encoder(): pl.pallas_call(functools.partial(kernel, layers, half, row_len), out_shap...]
    ppermute x24 -> x0, waiting for transfers between devices: 31.4 us -> none  [the longest x12 22.9 us: add_halo(): from_prev = lax.ppermute(tail_edge, axis_name, to_next)]
    conv_general_dilated x6 -> x0, matrix products: 7.87 us -> none  [conv_relu(): lax.conv_general_dilated(padded, weight, (stride, stride), 'VALID', dimen...]
  transfers between devices with their start and end apart: 24 -> 0, of which waited for: 16 -> 0; matrix products, arithmetic and copies ran while one was open for 1% -> 0% of each run, Pallas kernels for 0% -> 0%
where the time goes in v1:
time: 52 us; the launch traced here: 51.8 us
  Pallas kernels  50.4 us (97%)
  local copies, waits for them, and re-layouts  1.47 us (3%)
    pallas_call x1, Pallas kernels, local_encoder(): pl.pallas_call(functools.partial(kernel, layers, half, row_len), out_shap...  50.4 us
    unnamed x1, local copies, waits for them, and re-layouts  1.47 us

profile of v1, /device:TPU:97, one launch (start us, length us, event | category | flops | bytes accessed | tf_op | source)
XLA Modules:
  0.0 51.8 jit_solution(9402971554045482440)
XLA Ops:
  0.0 50.4 %encoder.1 = bf16[16,1,8,256]{3,2,1,0:T(8,128)(2,1)} custom-call(bf16[16,8,64,128]{3,2,1,0:T(8,128)(2,1)} %refs_0_.1, bf16[4,512,256]{2,1,0:T(8,128)(2,1)} %bitcast.17, f32[1,256]{1,0:T(1,128)} %bitcast.18, bf16[3,768,256]{2,1,0:T(8,128)(2,1)} %bitcast.14, f32[1,256]{1,0:T(1,128)} %bitcast.19, bf16[4,1024,256]{2,1,0:T(8,128)(2,1)} %bitcast.12, ...), custom_call_target="tpu_custom_call" | custom-call | tf_op jit(solution)/shard_map/encoder/pallas_call | solution.py:327
  50.4 1.5 %copy.15 = bf16[16,1,8,256]{3,2,1,0:T(8,128)(2,1)} copy(bf16[16,1,8,256]{3,2,1,0:T(8,128)(2,1)} %encoder.1) | data formatting | bytes 131072

commit v2 on v1

v2 whole, which is shorter than its diff:
```python
import functools

import jax
import jax.numpy as jnp
from jax import lax
from jax.experimental import pallas as pl
from jax.experimental.pallas import tpu as pltpu
from jax.sharding import PartitionSpec as P

MESH = pl.DeviceIdType.MESH
LANES = 128
PAD = 8

GROUP = (1, 1, 2, 2, 4)
PHASES = ((0,), (1,), (2,), (3, 4), (5,))
EXT_IN = (1, 1, 1, 2, 1, 1)
EXT_OUT = (0, 0, 0, 1, 0, 0)
LAST = len(PHASES) - 1


def plan(images, rows, width, c_in, c_out):
    layers = []
    for i in range(6):
        stride, taps = ((2, 4), (1, 3))[i % 2]
        phase = [p for p in range(len(PHASES)) if i in PHASES[p]][0]
        layers.append(
            dict(
                stride=stride, taps=taps, rows=rows, width=width, chan=c_in, out_rows=rows // stride, out_width=width // stride,
                ext=EXT_IN[i], ext_out=EXT_OUT[i], group=min(GROUP[phase], images),
            )
        )
        rows, width, c_in = rows // stride, width // stride, c_out
    return layers


def kernel(layers, half, row_len, *refs):
    images_ref = refs[0]
    w_hbm, b_hbm = refs[1:13:2], refs[2:14:2]
    out_ref = refs[13]
    refs = refs[14:]
    ximg, xedge, xhalo, feat = refs[:4]
    w_refs, b_refs = refs[4:10], refs[10:16]
    a_refs = refs[16:22]
    s_refs = refs[22:28]
    refs = refs[28:]
    send_bufs, halo_bufs = refs[:LAST], refs[LAST : 2 * LAST]
    refs = refs[2 * LAST :]
    w_sem, b_sem, own_sem, part_send, part_recv, load_sem, edge_send, edge_recv, out_sem = refs[:9]
    y_send, y_recv = refs[9 : 9 + LAST], refs[9 + LAST :]

    k = lax.axis_index("col")
    row = lax.axis_index("row")
    has = (row > 0, row < row_len - 1)
    near = (jnp.maximum(row - 1, 0), jnp.minimum(row + 1, row_len - 1))
    col_half = layers[0]["width"] // 2
    last_row = layers[0]["rows"] - 1
    g0 = layers[0]["group"]
    n_groups0 = half // g0

    barrier = pltpu.get_barrier_semaphore()
    for d in range(2):
        @pl.when(has[d])
        def _():
            for c in range(2):
                pl.semaphore_signal(barrier, inc=1, device_id={"col": c, "row": near[d]}, device_id_type=MESH)
    pl.semaphore_signal(barrier, inc=1, device_id={"col": 1 - k}, device_id_type=MESH)

    def edge_load(d):
        return pltpu.make_async_copy(images_ref.at[:, 0 if d == 0 else last_row], xedge.at[d], load_sem.at[d])

    def own_copy(g):
        src = images_ref.at[pl.ds(k * half + g * g0, g0)]
        return pltpu.make_async_copy(src, ximg.at[k, pl.ds(g * g0, g0)], own_sem.at[g])

    def part_copy(g):
        src = images_ref.at[pl.ds((1 - k) * half + g * g0, g0)]
        return pltpu.make_async_remote_copy(
            src, ximg.at[k, pl.ds(g * g0, g0)], part_send.at[g], part_recv.at[g], device_id={"col": 1 - k}, device_id_type=MESH
        )

    def part_arrival(g):
        dst = ximg.at[1 - k, pl.ds(g * g0, g0)]
        return pltpu.make_async_remote_copy(
            dst, dst, part_send.at[g], part_recv.at[g], device_id={"col": 1 - k}, device_id_type=MESH
        )

    def edge_copy(d, c, g):
        return pltpu.make_async_remote_copy(
            xedge.at[d, pl.ds(c * half + g * g0, g0)],
            xhalo.at[1 - d, k, pl.ds(g * g0, g0)],
            edge_send.at[d, c, g],
            edge_recv.at[1 - d, k, g],
            device_id={"col": c, "row": near[d]},
            device_id_type=MESH,
        )

    def edge_arrival(d, c, g):
        dst = xhalo.at[d, c, pl.ds(g * g0, g0)]
        return pltpu.make_async_remote_copy(
            dst, dst, edge_send.at[d, c, g], edge_recv.at[d, c, g], device_id={"col": c, "row": near[d]}, device_id_type=MESH
        )

    def y_copy(x, d, g):
        n = layers[PHASES[x][0]]["group"]
        return pltpu.make_async_remote_copy(
            send_bufs[x].at[d, pl.ds(g * n, n)],
            halo_bufs[x].at[1 - d, pl.ds(g * n, n)],
            y_send[x].at[d, g],
            y_recv[x].at[1 - d, g],
            device_id={"row": near[d]},
            device_id_type=MESH,
        )

    def y_arrival(x, d, g):
        n = layers[PHASES[x][0]]["group"]
        dst = halo_bufs[x].at[d, pl.ds(g * n, n)]
        return pltpu.make_async_remote_copy(
            dst, dst, y_send[x].at[d, g], y_recv[x].at[d, g], device_id={"row": near[d]}, device_id_type=MESH
        )

    def w_copy(i):
        return pltpu.make_async_copy(w_hbm[i], w_refs[i], w_sem.at[i])

    def b_copy(i):
        return pltpu.make_async_copy(b_hbm[i], b_refs[i], b_sem.at[i])

    for d in range(2):
        edge_load(d).start()
    own_copy(0).start()
    w_copy(0).start()
    for g in range(1, n_groups0):
        own_copy(g).start()
    for i in range(6):
        b_copy(i).start()

    for d in range(2):
        edge_load(d).wait()
    pl.semaphore_wait(barrier, 1 + 2 * (has[0].astype(jnp.int32) + has[1].astype(jnp.int32)))

    for g in range(n_groups0):
        for d in range(2):
            @pl.when(has[d])
            def _():
                for c in range(2):
                    edge_copy(d, c, g).start()
        part_copy(g).start()
    for i in range(1, 6):
        w_copy(i).start()

    for i, layer in enumerate(layers):
        w = layer["width"]
        s = s_refs[i]
        edge = jnp.zeros(s.shape[:-2] + (PAD, LANES), jnp.float32)
        s[..., pl.ds(0, PAD), :] = edge
        s[..., pl.ds(PAD + w, PAD), :] = edge
    for d in range(2):
        @pl.when(jnp.logical_not(has[d]))
        def _():
            xhalo[d] = jnp.zeros(xhalo.shape[1:], xhalo.dtype)
            for h in halo_bufs:
                h[d] = jnp.zeros(h.shape[1:], h.dtype)

    def taps_from(i, slot, img, rows):
        layer = layers[i]
        s, a = s_refs[i], a_refs[i]
        chan, w, stride = layer["chan"], layer["out_width"], layer["stride"]
        tiles = [(q, h) for q in range(layer["taps"]) for h in range(chan // LANES)]
        for r in rows:
            for t in range(0, len(tiles), 2):
                pair = []
                for q, h in tiles[t : t + 2]:
                    at = pl.ds(PAD - 1 + q, w) if stride == 1 else pl.ds(PAD - 1 + q, w, stride=2)
                    pair.append(s[slot, h, r, at, :])
                v = jnp.concatenate(pair, axis=-1).astype(jnp.bfloat16)
                lanes = pl.ds(t * LANES, 2 * LANES)
                if stride == 1:
                    a[img, r, :, lanes] = v
                else:
                    a[img, r % 2, r // 2, :, lanes] = v

    def product(i, first, chunk):
        layer = layers[i]
        a, out_rows = a_refs[i], layer["out_rows"] + 2 * layer["ext_out"]
        acc = None
        for p in range(layer["taps"]):
            if layer["stride"] == 1:
                left = a[pl.ds(first, chunk), pl.ds(p, out_rows)]
            else:
                left = a[pl.ds(first, chunk), p % 2, pl.ds(p // 2, out_rows)]
            left = left.reshape(chunk * out_rows * layer["out_width"], left.shape[-1])
            part = jnp.dot(left, w_refs[i][p], preferred_element_type=jnp.float32)
            acc = part if acc is None else acc + part
        v = jnp.maximum(acc + b_refs[i][...], 0.0)
        return v.reshape(chunk, out_rows, layer["out_width"], v.shape[-1])

    def keep_rows(i, slot, v, r):
        w = layers[i]["width"]
        for h in range(v.shape[-1] // LANES):
            s_refs[i][slot, h, pl.ds(r, v.shape[0]), pl.ds(PAD, w), :] = v[:, :, h * LANES : (h + 1) * LANES]

    def phase_step(phase, g):
        first = layers[PHASES[phase][0]]
        n = first["group"]
        base = g * n
        if phase == 0:
            own_copy(g).wait()
            part_arrival(g).wait_recv()
            for d in range(2):
                @pl.when(has[d])
                def _():
                    for c in range(2):
                        edge_arrival(d, c, g).wait_recv()
        else:
            before = layers[PHASES[phase - 1][0]]["group"]
            for d in range(2):
                @pl.when(has[d])
                def _():
                    for j in range(n // before):
                        y_arrival(phase - 1, d, g * (n // before) + j).wait_recv()

        for j in range(n):
            img = base + j
            if phase == 0:
                rows = first["rows"]
                for c in range(2):
                    at = pl.ds(PAD + c * col_half, col_half)
                    s = s_refs[0]
                    s[j, 0, 0, at, :] = xhalo[0, c, img].astype(jnp.float32)
                    s[j, 0, pl.ds(1, rows), at, :] = ximg[c, img].astype(jnp.float32)
                    s[j, 0, rows + 1, at, :] = xhalo[1, c, img].astype(jnp.float32)
                taps_from(0, j, j, range(rows + 2))
            else:
                i, ext = PHASES[phase][0], first["ext"]
                for d, r in ((0, 0), (1, first["rows"] + ext)):
                    keep_rows(i, j, halo_bufs[phase - 1][d, img].astype(jnp.float32), r)
                    taps_from(i, j, img, range(r, r + ext))

        for i in PHASES[phase]:
            layer = layers[i]
            local = i != PHASES[phase][0] or i == 0
            chunk = n if i >= 2 else 1
            for m in range(0, n, chunk):
                v = product(i, m if local else base + m, chunk)
                if i == 5:
                    w = layer["out_width"]
                    for c in range(2):
                        feat[c, pl.ds(base + m, chunk)] = v[:, 0, c * w // 2 : (c + 1) * w // 2].astype(jnp.bfloat16)
                    continue
                ext, out_rows = layer["ext_out"], layer["out_rows"]
                if i == PHASES[phase][-1]:
                    x = phase
                    depth = send_bufs[x].shape[2]
                    for d, r in ((0, 0), (1, out_rows - depth)):
                        send_bufs[x][d, pl.ds(base + m, chunk)] = v[:, r : r + depth].astype(jnp.bfloat16)
                    slots = s_refs[i + 1].shape[0]
                    r0 = layers[i + 1]["ext"]
                    for j in range(chunk):
                        slot = (m + j) % slots
                        keep_rows(i + 1, slot, v[j], r0)
                        taps_from(i + 1, slot, base + m + j, range(r0, r0 + out_rows))
                else:
                    for j in range(chunk):
                        slot = m + j
                        keep_rows(i + 1, slot, jnp.where(has[0], v[j, :ext], 0.0), 0)
                        keep_rows(i + 1, slot, v[j, ext : ext + out_rows], ext)
                        keep_rows(i + 1, slot, jnp.where(has[1], v[j, ext + out_rows :], 0.0), ext + out_rows)
                        taps_from(i + 1, slot, slot, range(out_rows + 2 * ext))
        if phase < LAST:
            for d in range(2):
                @pl.when(has[d])
                def _():
                    y_copy(phase, d, g).start()

    for phase in range(LAST + 1):
        for i in PHASES[phase]:
            w_copy(i).wait()
            b_copy(i).wait()
        groups = half // layers[PHASES[phase][0]]["group"]
        if groups == 1:
            phase_step(phase, 0)
        else:
            @pl.loop(0, groups)
            def _(g):
                phase_step(phase, g)

    mine = pltpu.make_async_copy(feat.at[k], out_ref.at[pl.ds(k * half, half), 0], out_sem.at[0])
    theirs = pltpu.make_async_remote_copy(
        feat.at[1 - k],
        out_ref.at[pl.ds(k * half, half), 0],
        out_sem.at[1],
        out_sem.at[2],
        device_id={"col": 1 - k},
        device_id_type=MESH,
    )
    arriving = pltpu.make_async_remote_copy(
        feat.at[1 - k],
        out_ref.at[pl.ds((1 - k) * half, half), 0],
        out_sem.at[1],
        out_sem.at[2],
        device_id={"col": 1 - k},
        device_id_type=MESH,
    )
    theirs.start()
    mine.start()

    for g in range(n_groups0):
        part_copy(g).wait_send()
        for d in range(2):
            @pl.when(has[d])
            def _():
                for c in range(2):
                    edge_copy(d, c, g).wait_send()
    for x in range(LAST):
        for g in range(half // layers[PHASES[x][0]]["group"]):
            for d in range(2):
                @pl.when(has[d])
                def _():
                    y_copy(x, d, g).wait_send()
    mine.wait()
    theirs.wait_send()
    arriving.wait_recv()


def solution(mesh):
    row_len = mesh.shape["row"]

    def local_encoder(images, *params):
        n_img, rows, col_half, c_in = images.shape
        half = n_img // 2
        weights, biases = params[0::2], params[1::2]
        c_out = weights[0].shape[-1]
        layers = plan(half, rows, 2 * col_half, c_in, c_out)
        args = [images]
        for w, b in zip(weights, biases):
            args += [w.reshape(w.shape[0], w.shape[1] * w.shape[2], c_out), b.reshape(1, c_out)]

        bf16, f32 = jnp.bfloat16, jnp.float32
        scratch = [
            pltpu.VMEM((2, half, rows, col_half, c_in), bf16),
            pltpu.VMEM((2, n_img, col_half, c_in), bf16),
            pltpu.VMEM((2, 2, half, col_half, c_in), bf16),
            pltpu.VMEM((2, half, layers[5]["out_width"] // 2, c_out), bf16),
        ]
        scratch += [pltpu.VMEM(w.shape, bf16) for w in args[1::2]]
        scratch += [pltpu.VMEM((1, c_out), f32) for _ in biases]
        for i, la in enumerate(layers):
            held = half if i in [p[0] for p in PHASES[1:]] else la["group"]
            depth = la["taps"] * la["chan"]
            total = la["rows"] + 2 * la["ext"]
            if la["stride"] == 1:
                shape = (held, total, la["out_width"], depth)
            else:
                shape = (held, 2, total // 2, la["out_width"], depth)
            scratch.append(pltpu.VMEM(shape, bf16))
        for la in layers:
            total = la["rows"] + 2 * la["ext"]
            scratch.append(pltpu.VMEM((la["group"], la["chan"] // LANES, total, la["width"] + 3 * PAD, LANES), f32))
        edges = [pltpu.VMEM((2, half, layers[i]["ext"], layers[i]["width"], c_out), bf16) for i in [p[0] for p in PHASES[1:]]]
        scratch += edges + edges
        dma = pltpu.SemaphoreType.DMA
        g0 = half // layers[0]["group"]
        scratch += [dma((6,)), dma((6,)), dma((g0,)), dma((g0,)), dma((g0,)), dma((2,)), dma((2, 2, g0)), dma((2, 2, g0)), dma((3,))]
        sems = [dma((2, half // layers[i]["group"])) for i in [p[0] for p in PHASES[:-1]]]
        scratch += sems + sems

        any_spec = pl.BlockSpec(memory_space=pl.ANY)
        return pl.pallas_call(
            functools.partial(kernel, layers, half, row_len),
            out_shape=jax.ShapeDtypeStruct((n_img, rows // 8, col_half // 8, c_out), bf16),
            in_specs=[any_spec] * len(args),
            out_specs=any_spec,
            scratch_shapes=scratch,
            compiler_params=pltpu.CompilerParams(collective_id=0, has_side_effects=True, vmem_limit_bytes=60 * 1024 * 1024),
            name="encoder",
        )(*args)

    tile_spec = P("batch", "row", "col", None)
    return jax.shard_map(local_encoder, mesh=mesh, in_specs=(tile_spec,) + (P(),) * 12, out_specs=tile_spec, check_vma=False)
```

time: 52 us -> 44.6 us (0.86)
  Pallas kernels: 50.4 us -> 43 us
    pallas_call x1, Pallas kernels: 50.4 us -> 43 us  [local_encoder(): pl.pallas_call(functools.partial(kernel, layers, half, row_len), out_shap...]
where the time goes in v2:
time: 44.6 us; the launch traced here: 44.5 us
  Pallas kernels  43 us (96%)
  local copies, waits for them, and re-layouts  1.47 us (3%)
    pallas_call x1, Pallas kernels, local_encoder(): pl.pallas_call(functools.partial(kernel, layers, half, row_len), out_shap...  43 us
    unnamed x1, local copies, waits for them, and re-layouts  1.47 us

profile of v2, /device:TPU:97, one launch (start us, length us, event | category | flops | bytes accessed | tf_op | source)
XLA Modules:
  0.0 44.5 jit_solution(4535071439733901064)
XLA Ops:
  0.0 43.0 %encoder.1 = bf16[16,1,8,256]{3,2,1,0:T(8,128)(2,1)} custom-call(bf16[16,8,64,128]{3,2,1,0:T(8,128)(2,1)} %refs_0_.1, bf16[4,512,256]{2,1,0:T(8,128)(2,1)} %bitcast.17, f32[1,256]{1,0:T(1,128)} %bitcast.18, bf16[3,768,256]{2,1,0:T(8,128)(2,1)} %bitcast.14, f32[1,256]{1,0:T(1,128)} %bitcast.19, bf16[4,1024,256]{2,1,0:T(8,128)(2,1)} %bitcast.12, ...), custom_call_target="tpu_custom_call" | custom-call | tf_op jit(solution)/shard_map/encoder/pallas_call | solution.py:367
  43.0 1.5 %copy.15 = bf16[16,1,8,256]{3,2,1,0:T(8,128)(2,1)} copy(bf16[16,1,8,256]{3,2,1,0:T(8,128)(2,1)} %encoder.1) | data formatting | bytes 131072

commit v3 on v0

v3 whole, which is shorter than its diff:
```python
import functools

import jax
import jax.numpy as jnp
from jax import lax
from jax.experimental import pallas as pl
from jax.experimental.pallas import tpu as pltpu
from jax.sharding import PartitionSpec as P

MESH = pl.DeviceIdType.MESH
LANES = 128
PAD = 8
RING = 4

LAYERS = ((2, 4, 1), (1, 3, 2), (2, 4, 1), (1, 3, 4), (2, 4, 3), (1, 3, 1))
BF16, F32 = jnp.bfloat16, jnp.float32


def kernel(half, row_len, *refs):
    images_ref = refs[0]
    w_hbm, b_hbm = refs[1:13:2], refs[2:14:2]
    out_ref = refs[13]
    refs = refs[14:]
    ximg, xedge, xhalo, y_out, y_in, y_halo, u_out, u_halo, f_out, f_in = refs[:10]
    w_refs, b_refs, a_refs, s_refs = refs[10:16], refs[16:22], refs[22:28], refs[28:34]
    (w_sem, b_sem, own_sem, part_send, part_recv, load_sem, edge_send, edge_recv) = refs[34:42]
    (y_send, y_recv, yh_send, yh_recv, u_send, u_recv, f_send, f_recv) = refs[42:]

    k = lax.axis_index("col")
    row = lax.axis_index("row")
    x = row % RING
    first = row - x
    per = half // RING
    has = (row > 0, row < row_len - 1)
    near = (jnp.maximum(row - 1, 0), jnp.minimum(row + 1, row_len - 1))
    has_block = (row >= RING, row < row_len - RING)
    near_block = (jnp.maximum(row - RING, 0), jnp.minimum(row + RING, row_len - 1))
    tile_rows = ximg.shape[2]
    col_half = ximg.shape[3]
    y_part = y_out.shape[2]
    y_rows = 2 * y_part

    barrier = pltpu.get_barrier_semaphore()
    crosses = (jnp.logical_and(has[0], x == 0), jnp.logical_and(has[1], x == RING - 1))
    for d in range(2):
        @pl.when(crosses[d])
        def _():
            for c in range(2):
                pl.semaphore_signal(barrier, inc=1, device_id={"col": c, "row": near[d]}, device_id_type=MESH)

        @pl.when(has_block[d])
        def _():
            pl.semaphore_signal(barrier, inc=1, device_id={"row": near_block[d]}, device_id_type=MESH)
    for o in (2, 1, 3):
        for c in range(2):
            pl.semaphore_signal(barrier, inc=1, device_id={"col": c, "row": first + (x + o) % RING}, device_id_type=MESH)
    pl.semaphore_signal(barrier, inc=1, device_id={"col": 1 - k}, device_id_type=MESH)

    def turn(i, at):
        step, pair = i % RING, (i % RING) // 2
        offset = (1 - pair) * (2 + step) + pair * (3 - step)
        return (i // RING) * RING + (at + offset) % RING

    def edge_load(d):
        return pltpu.make_async_copy(images_ref.at[:, 0 if d == 0 else tile_rows - 1], xedge.at[d], load_sem.at[d])

    def own_copy(j):
        return pltpu.make_async_copy(images_ref.at[k * half + j], ximg.at[k, j], own_sem.at[j])

    def part_copy(j):
        return pltpu.make_async_remote_copy(
            images_ref.at[(1 - k) * half + j], ximg.at[k, j], part_send.at[j], part_recv.at[j],
            device_id={"col": 1 - k}, device_id_type=MESH,
        )

    def part_arrival(j):
        dst = ximg.at[1 - k, j]
        return pltpu.make_async_remote_copy(
            dst, dst, part_send.at[j], part_recv.at[j], device_id={"col": 1 - k}, device_id_type=MESH
        )

    def edge_copy(d, c, j):
        return pltpu.make_async_remote_copy(
            xedge.at[d, c * half + j], xhalo.at[1 - d, k, j], edge_send.at[d, c, j], edge_recv.at[1 - d, k, j],
            device_id={"col": c, "row": near[d]}, device_id_type=MESH,
        )

    def edge_arrival(d, c, j):
        dst = xhalo.at[d, c, j]
        return pltpu.make_async_remote_copy(
            dst, dst, edge_send.at[d, c, j], edge_recv.at[d, c, j], device_id={"col": c, "row": near[d]}, device_id_type=MESH
        )

    def y_copy(j, e):
        return pltpu.make_async_remote_copy(
            y_out.at[j, e], y_in.at[j // RING, x, e], y_send.at[j, e], y_recv.at[j // RING, x, e],
            device_id={"row": first + j % RING}, device_id_type=MESH,
        )

    def y_stays(j, e):
        return pltpu.make_async_copy(y_out.at[j, e], y_in.at[j // RING, x, e], y_recv.at[j // RING, x, e])

    def y_leaves(j, e):
        stays = j % RING == x

        @pl.when(stays)
        def _():
            y_stays(j, e).start()

        @pl.when(jnp.logical_not(stays))
        def _():
            y_copy(j, e).start()

    def y_arrival(r, src, e):
        dst = y_in.at[r, src, e]
        return pltpu.make_async_copy(dst, dst, y_recv.at[r, src, e])

    def block_copy(src, halo, d, r, send, recv):
        return pltpu.make_async_remote_copy(
            src, halo.at[1 - d, r], send.at[d, r], recv.at[1 - d, r], device_id={"row": near_block[d]}, device_id_type=MESH
        )

    def yh_copy(d, r):
        return block_copy(y_in.at[r, d * (RING - 1), d], y_halo, d, r, yh_send, yh_recv)

    def u_copy(d, r):
        return block_copy(u_out.at[d, r], u_halo, d, r, u_send, u_recv)

    def block_arrival(halo, d, r, send, recv):
        dst = halo.at[d, r]
        return pltpu.make_async_remote_copy(
            dst, dst, send.at[d, r], recv.at[d, r], device_id={"row": near_block[d]}, device_id_type=MESH
        )

    def f_copy(o, c):
        to = (x + o) % RING
        return pltpu.make_async_remote_copy(
            f_out.at[to, c], f_in.at[k, x], f_send.at[o, c], f_recv.at[k, x],
            device_id={"col": c, "row": first + to}, device_id_type=MESH,
        )

    def f_stays():
        return pltpu.make_async_copy(f_out.at[x, k], f_in.at[k, x], f_recv.at[k, x])

    def f_arrival(c, src):
        dst = f_in.at[c, src]
        return pltpu.make_async_copy(dst, dst, f_recv.at[c, src])

    def w_copy(i):
        return pltpu.make_async_copy(w_hbm[i], w_refs[i], w_sem.at[i])

    def b_copy(i):
        return pltpu.make_async_copy(b_hbm[i], b_refs[i], b_sem.at[i])

    for d in range(2):
        edge_load(d).start()
    for i in range(half):
        own_copy(turn(i, x)).start()
        if i == 0:
            w_copy(0).start()
    for i in range(6):
        b_copy(i).start()

    for (stride, _, _), s in zip(LAYERS, s_refs):
        w = s.shape[-2] - 3 * PAD
        edge = jnp.zeros(s.shape[:-2] + (PAD, LANES), F32)
        s[..., pl.ds(0, PAD), :] = edge
        s[..., pl.ds(PAD + w, PAD), :] = edge
    for d in range(2):
        @pl.when(jnp.logical_not(has[d]))
        def _():
            xhalo[d] = jnp.zeros(xhalo.shape[1:], BF16)

        @pl.when(jnp.logical_not(has_block[d]))
        def _():
            y_halo[d] = jnp.zeros(y_halo.shape[1:], BF16)
            u_halo[d] = jnp.zeros(u_halo.shape[1:], BF16)

    for d in range(2):
        edge_load(d).wait()
    count = 2 * RING - 1
    for d in range(2):
        count = count + 2 * crosses[d].astype(jnp.int32) + has_block[d].astype(jnp.int32)
    pl.semaphore_wait(barrier, count)

    for i in range(half):
        part_copy(turn(i, x)).start()
        for d in range(2):
            @pl.when(has[d])
            def _():
                for c in range(2):
                    edge_copy(d, c, turn(i, (x + 2 * d - 1) % RING)).start()
    for i in range(1, 6):
        w_copy(i).start()

    def keep(i, v, r):
        s = s_refs[i]
        w = s.shape[-2] - 3 * PAD
        for h in range(v.shape[-1] // LANES):
            s[h, pl.ds(r, v.shape[0]), pl.ds(PAD, w), :] = v[:, :, h * LANES : (h + 1) * LANES]

    def spread(i, rows, a):
        stride, taps, _ = LAYERS[i]
        s = s_refs[i]
        w = (s.shape[-2] - 3 * PAD) // stride
        tiles = [(q, h) for q in range(taps) for h in range(s.shape[0])]
        for r in rows:
            for t in range(0, len(tiles), 2):
                pair = []
                for q, h in tiles[t : t + 2]:
                    at = pl.ds(PAD - 1 + q, w) if stride == 1 else pl.ds(PAD - 1 + q, w, stride=2)
                    pair.append(s[h, r, at, :])
                v = jnp.concatenate(pair, axis=-1).astype(BF16)
                lanes = pl.ds(t * LANES, 2 * LANES)
                if stride == 1:
                    a[r, :, lanes] = v
                else:
                    a[r % 2, r // 2, :, lanes] = v

    def product(i, a, o, n):
        stride, taps, _ = LAYERS[i]
        acc = None
        for p in range(taps):
            left = a[pl.ds(o + p, n)] if stride == 1 else a[p % 2, pl.ds(o + p // 2, n)]
            _, w, depth = left.shape
            part = jnp.dot(left.reshape(n * w, depth), w_refs[i][p], preferred_element_type=F32)
            acc = part if acc is None else acc + part
        v = jnp.maximum(acc + b_refs[i][...], 0.0)
        return v.reshape(n, w, v.shape[-1])

    def inside(v, d):
        return jnp.where(has_block[d], v, 0.0)

    def first_step(i):
        j = turn(i, x)
        own_copy(j).wait()
        part_arrival(j).wait_recv()
        for d in range(2):
            @pl.when(has[d])
            def _():
                for c in range(2):
                    edge_arrival(d, c, j).wait_recv()
        s = s_refs[0]
        for c in range(2):
            at = pl.ds(PAD + c * col_half, col_half)
            s[0, 0, at, :] = xhalo[0, c, j].astype(F32)
            s[0, pl.ds(1, tile_rows), at, :] = ximg[c, j].astype(F32)
            s[0, tile_rows + 1, at, :] = xhalo[1, c, j].astype(F32)
        spread(0, range(tile_rows + 2), a_refs[0])
        for e in range(2):
            y_out[j, e] = product(0, a_refs[0], e * y_part, y_part).astype(BF16)
        edge = x // (RING - 1)
        y_leaves(j, edge)

        @pl.when(i >= half - RING)
        def _():
            y_leaves(turn(i - half + RING, x), 1 - edge)

    def forward(r):
        for d in range(2):
            y_arrival(r, d * (RING - 1), d).wait()

            @pl.when(has_block[d])
            def _():
                yh_copy(d, r).start()

    def second_step(r):
        a1, a2, a3 = a_refs[1], a_refs[2], a_refs[3].at[r]
        for src in range(RING):
            for e in range(2):
                if (src, e) not in ((0, 0), (RING - 1, 1)):
                    y_arrival(r, src, e).wait()
        for d in range(2):
            @pl.when(has_block[d])
            def _():
                block_arrival(y_halo, d, r, yh_send, yh_recv).wait_recv()
        own = RING * y_rows
        keep(1, y_halo[0, r].astype(F32), 0)
        for src in range(RING):
            for e in range(2):
                keep(1, y_in[r, src, e].astype(F32), 2 + src * y_rows + e * y_part)
        keep(1, y_halo[1, r].astype(F32), 2 + own)
        n = 3
        for o in range(0, own + 2, n):
            spread(1, range(o if o == 0 else o + 2, o + n + 2), a1)
            v = product(1, a1, o, n)
            if o == 0:
                keep(2, inside(v[:1], 0), 0)
                keep(2, v[1:], 1)
            elif o == own + 2 - n:
                keep(2, v[: n - 1], o)
                keep(2, inside(v[n - 1 :], 1), own + 1)
            else:
                keep(2, v, o)
            spread(2, range(o, o + n), a2)

        u_rows = own // 2
        depth = u_halo.shape[2]
        n = u_rows // 2
        for e in range(2):
            v = product(2, a2, e * n, n)
            u_out[e, r] = v.astype(BF16)
            keep(3, v, depth + e * n)
        for d in range(2):
            @pl.when(has_block[d])
            def _():
                u_copy(d, r).start()
        spread(3, range(depth, depth + u_rows), a3)

    def third_step(r):
        a3, a4, a5 = a_refs[3].at[r], a_refs[4], a_refs[5]
        depth = u_halo.shape[2]
        u_rows = RING * y_rows // 2
        n = (u_rows - 2) // 2
        for o in (depth, depth + n):
            keep(4, product(3, a3, o, n), o)
        spread(4, range(depth, depth + u_rows - 2), a4)
        for d in range(2):
            @pl.when(has_block[d])
            def _():
                block_arrival(u_halo, d, r, u_send, u_recv).wait_recv()
        for d, o in ((0, 0), (1, depth + u_rows)):
            keep(3, u_halo[d, r].astype(F32), o)
            spread(3, range(o, o + depth), a3)
        low = depth + u_rows - 2
        v = product(3, a3, 0, depth)
        keep(4, inside(v[: depth - 1], 0), 0)
        keep(4, v[depth - 1 :], depth - 1)
        v = product(3, a3, low, depth)
        keep(4, v[:1], low)
        keep(4, inside(v[1:], 1), low + 1)
        for o in (0, low):
            spread(4, range(o, o + depth), a4)
        f_rows = u_rows // 2
        v = product(4, a4, 0, f_rows + 2)
        keep(5, inside(v[:1], 0), 0)
        keep(5, v[1 : 1 + f_rows], 1)
        keep(5, inside(v[1 + f_rows :], 1), 1 + f_rows)
        spread(5, range(f_rows + 2), a5)
        v = product(5, a5, 0, f_rows)
        w = v.shape[1] // 2
        for t in range(f_rows):
            for c in range(2):
                f_out[t, c, r] = v[t, c * w : (c + 1) * w].astype(BF16)

    def ready(i):
        w_copy(i).wait()
        b_copy(i).wait()

    ready(0)
    pl.loop(0, half)(first_step)
    for i in range(half - RING, half):
        y_leaves(turn(i, x), 1 - x // (RING - 1))
    ready(1)
    ready(2)
    for r in range(per):
        forward(r)
    pl.loop(0, per)(second_step)
    for i in (3, 4, 5):
        ready(i)
    pl.loop(0, per)(third_step)

    for o in (2, 1, 3, 0):
        for c in range(2):
            if o:
                f_copy(o, c).start()
            else:
                @pl.when(k == c)
                def _():
                    f_stays().start()

                @pl.when(k != c)
                def _():
                    f_copy(0, c).start()

    for i in range(half):
        part_copy(turn(i, x)).wait_send()
        for d in range(2):
            @pl.when(has[d])
            def _():
                for c in range(2):
                    edge_copy(d, c, turn(i, (x + 2 * d - 1) % RING)).wait_send()
        if i % RING != RING - 1:
            for e in range(2):
                y_copy(turn(i, x), e).wait_send()
    for r in range(per):
        for d in range(2):
            @pl.when(has_block[d])
            def _():
                yh_copy(d, r).wait_send()
                u_copy(d, r).wait_send()
    for o in range(RING):
        for c in range(2):
            if o:
                f_copy(o, c).wait_send()
            else:
                @pl.when(k != c)
                def _():
                    f_copy(0, c).wait_send()
    for c in range(2):
        for src in range(RING):
            f_arrival(c, src).wait()
            for r in range(per):
                out_ref[c * half + r * RING + src, 0] = f_in[c, src, r]


def solution(mesh):
    row_len = mesh.shape["row"]

    def local_encoder(images, *params):
        n_img, rows, col_half, c_in = images.shape
        half = n_img // 2
        per = half // RING
        weights, biases = params[0::2], params[1::2]
        c_out = weights[0].shape[-1]
        args = [images]
        for w, b in zip(weights, biases):
            args += [w.reshape(w.shape[0], w.shape[1] * w.shape[2], c_out), b.reshape(1, c_out)]

        y_rows, u_rows, f_rows = rows // 2, RING * rows // 4, RING * rows // 8
        width = 2 * col_half
        depth1, depth3 = LAYERS[1][2], LAYERS[3][2]
        vmem, dma = pltpu.VMEM, pltpu.SemaphoreType.DMA
        scratch = [
            vmem((2, half, rows, col_half, c_in), BF16),
            vmem((2, n_img, col_half, c_in), BF16),
            vmem((2, 2, half, col_half, c_in), BF16),
            vmem((half, 2, y_rows // 2, width // 2, c_out), BF16),
            vmem((per, RING, 2, y_rows // 2, width // 2, c_out), BF16),
            vmem((2, per, depth1, width // 2, c_out), BF16),
            vmem((2, per, depth3, width // 4, c_out), BF16),
            vmem((2, per, depth3, width // 4, c_out), BF16),
            vmem((f_rows, 2, per, width // 16, c_out), BF16),
            vmem((2, RING, per, width // 16, c_out), BF16),
        ]
        scratch += [vmem(w.shape, BF16) for w in args[1::2]]
        scratch += [vmem((1, c_out), F32) for _ in biases]
        held, spans = [], (rows, RING * y_rows, RING * y_rows, u_rows, u_rows, f_rows)
        for i, (stride, taps, ext) in enumerate(LAYERS):
            chan = c_in if i == 0 else c_out
            total, w = spans[i] + 2 * ext, width // (1, 2, 2, 4, 4, 8)[i]
            shape = (total, w, taps * chan) if stride == 1 else (2, total // 2, w // 2, taps * chan)
            scratch.append(vmem((per,) + shape if i == 3 else shape, BF16))
            held.append(vmem((chan // LANES, total, w + 3 * PAD, LANES), F32))
        scratch += held
        scratch += [dma((6,)), dma((6,)), dma((half,)), dma((half,)), dma((half,)), dma((2,)), dma((2, 2, half)), dma((2, 2, half))]
        scratch += [dma((half, 2)), dma((per, RING, 2))] + [dma((2, per))] * 4 + [dma((RING, 2)), dma((2, RING))]

        any_spec = pl.BlockSpec(memory_space=pl.ANY)
        return pl.pallas_call(
            functools.partial(kernel, half, row_len),
            out_shape=jax.ShapeDtypeStruct((n_img, rows // 8, col_half // 8, c_out), BF16),
            in_specs=[any_spec] * len(args),
            out_specs=pl.BlockSpec(memory_space=pltpu.VMEM),
            scratch_shapes=scratch,
            compiler_params=pltpu.CompilerParams(collective_id=0, has_side_effects=True, vmem_limit_bytes=56 * 1024 * 1024),
            name="encoder",
        )(*args)

    tile_spec = P("batch", "row", "col", None)
    return jax.shard_map(local_encoder, mesh=mesh, in_specs=(tile_spec,) + (P(),) * 12, out_specs=tile_spec, check_vma=False)
```

time: 136 us -> 41.8 us (0.31)
  starting transfers between devices: 91.3 us -> 0 us
  Pallas kernels: 0 us -> 40.2 us
  waiting for transfers between devices: 31.4 us -> 0 us
  matrix products: 7.87 us -> 0 us
  local copies, waits for them, and re-layouts: 4.04 us -> 1.47 us
    ppermute x24 -> x0, starting transfers between devices: 91.3 us -> none  [the longest x12 70.7 us: add_halo(): from_next = lax.ppermute(head_edge, axis_name, to_prev)]
    pallas_call x0 -> x1, Pallas kernels: none -> 40.2 us  [local_encoder(): pl.pallas_call(functools.partial(kernel, half, row_len), out_shape=jax.Sh...]
    ppermute x24 -> x0, waiting for transfers between devices: 31.4 us -> none  [the longest x12 22.9 us: add_halo(): from_prev = lax.ppermute(tail_edge, axis_name, to_next)]
    conv_general_dilated x6 -> x0, matrix products: 7.87 us -> none  [conv_relu(): lax.conv_general_dilated(padded, weight, (stride, stride), 'VALID', dimen...]
  transfers between devices with their start and end apart: 24 -> 0, of which waited for: 16 -> 0; matrix products, arithmetic and copies ran while one was open for 1% -> 0% of each run, Pallas kernels for 0% -> 0%
where the time goes in v3:
time: 41.8 us; the launch traced here: 41.6 us
  Pallas kernels  40.2 us (96%)
  local copies, waits for them, and re-layouts  1.47 us (4%)
    pallas_call x1, Pallas kernels, local_encoder(): pl.pallas_call(functools.partial(kernel, half, row_len), out_shape=jax.Sh...  40.2 us
    unnamed x1, local copies, waits for them, and re-layouts  1.47 us

profile of v3, /device:TPU:97, one launch (start us, length us, event | category | flops | bytes accessed | tf_op | source)
XLA Modules:
  0.0 41.6 jit_solution(6649334212686381578)
XLA Ops:
  0.0 40.2 %encoder.1 = bf16[16,1,8,256]{3,2,1,0:T(8,128)(2,1)} custom-call(bf16[16,8,64,128]{3,2,1,0:T(8,128)(2,1)} %refs_0_.1, bf16[4,512,256]{2,1,0:T(8,128)(2,1)} %bitcast.17, f32[1,256]{1,0:T(1,128)} %bitcast.18, bf16[3,768,256]{2,1,0:T(8,128)(2,1)} %bitcast.14, f32[1,256]{1,0:T(1,128)} %bitcast.19, bf16[4,1024,256]{2,1,0:T(8,128)(2,1)} %bitcast.12, ...), custom_call_target="tpu_custom_call" | custom-call | tf_op jit(solution)/shard_map/encoder/pallas_call | solution.py:450
  40.2 1.5 %copy.15 = bf16[16,1,8,256]{3,2,1,0:T(8,128)(2,1)} copy(bf16[16,1,8,256]{3,2,1,0:T(8,128)(2,1)} %encoder.1) | data formatting | bytes 131072

commit v4 on v3

v4 whole, which is shorter than its diff:
```python
import functools

import jax
import jax.numpy as jnp
from jax import lax
from jax.experimental import pallas as pl
from jax.experimental.pallas import tpu as pltpu
from jax.sharding import PartitionSpec as P

MESH = pl.DeviceIdType.MESH
LANES = 128
PAD = 8
RING = 4

LAYERS = ((2, 4, 1), (1, 3, 2), (2, 4, 1), (1, 3, 4), (2, 4, 3), (1, 3, 1))
BF16, F32 = jnp.bfloat16, jnp.float32


def kernel(half, row_len, *refs):
    images_ref = refs[0]
    w_hbm, b_hbm = refs[1:13:2], refs[2:14:2]
    out_ref = refs[13]
    refs = refs[14:]
    ximg, xedge, xhalo, y_out, y_in, y_halo, u_out, u_halo, f_out, f_in = refs[:10]
    w_refs, b_all, a_refs, s_refs = refs[10:16], refs[16], refs[17:23], refs[23:29]
    (w_sem, b_sem, in_sem, part_send, load_sem, edge_send, edge_recv, y_send, y_recv, yh_send, yh_recv, u_send, u_recv, f_send, f_recv) = refs[29:]

    k = lax.axis_index("col")
    row = lax.axis_index("row")
    x = row % RING
    first = row - x
    per = half // RING
    has = (row > 0, row < row_len - 1)
    near = (jnp.maximum(row - 1, 0), jnp.minimum(row + 1, row_len - 1))
    has_block = (row >= RING, row < row_len - RING)
    near_block = (jnp.maximum(row - RING, 0), jnp.minimum(row + RING, row_len - 1))
    tile_rows, col_half = ximg.shape[2:4]
    y_part = y_out.shape[2]
    y_rows = 2 * y_part

    barrier = pltpu.get_barrier_semaphore()
    crosses = (jnp.logical_and(has[0], x == 0), jnp.logical_and(has[1], x == RING - 1))
    for d in range(2):
        @pl.when(crosses[d])
        def _():
            for c in range(2):
                pl.semaphore_signal(barrier, inc=1, device_id={"col": c, "row": near[d]}, device_id_type=MESH)

        @pl.when(has_block[d])
        def _():
            pl.semaphore_signal(barrier, inc=1, device_id={"row": near_block[d]}, device_id_type=MESH)
    for o in (2, 1, 3):
        for c in range(2):
            pl.semaphore_signal(barrier, inc=1, device_id={"col": c, "row": first + (x + o) % RING}, device_id_type=MESH)
    pl.semaphore_signal(barrier, inc=1, device_id={"col": 1 - k}, device_id_type=MESH)

    def turn(i, at):
        step, pair = i % RING, (i % RING) // 2
        offset = (1 - pair) * (2 + step) + pair * (3 - step)
        return (i // RING) * RING + (at + offset) % RING

    def settle(ref, sem):
        pltpu.make_async_copy(ref, ref, sem).wait()

    def edge_load(d):
        return pltpu.make_async_copy(images_ref.at[:, 0 if d == 0 else tile_rows - 1], xedge.at[d], load_sem.at[0])

    def own_copy(j):
        return pltpu.make_async_copy(images_ref.at[k * half + j], ximg.at[j, k], in_sem.at[j])

    def part_copy(j):
        return pltpu.make_async_remote_copy(
            images_ref.at[(1 - k) * half + j], ximg.at[j, k], part_send.at[0], in_sem.at[j],
            device_id={"col": 1 - k}, device_id_type=MESH,
        )

    def edge_copy(d, c, j):
        return pltpu.make_async_remote_copy(
            xedge.at[d, c * half + j], xhalo.at[1 - d, j, k], edge_send.at[d], edge_recv.at[1 - d, j],
            device_id={"col": c, "row": near[d]}, device_id_type=MESH,
        )

    def y_kind(at, e):
        place = 2 * at + e
        return 2 * ((place + 2 * RING - 2) // (2 * RING - 1)) - place // (2 * RING - 1)

    def y_copy(j, e):
        return pltpu.make_async_remote_copy(
            y_out.at[j, e], y_in.at[j // RING, 2 * x + e], y_send.at[0], y_recv.at[j // RING, y_kind(x, e)],
            device_id={"row": first + j % RING}, device_id_type=MESH,
        )

    def y_stays(j, e):
        return pltpu.make_async_copy(y_out.at[j, e], y_in.at[j // RING, 2 * x + e], y_recv.at[j // RING, y_kind(x, e)])

    def y_leaves(j, e):
        stays = j % RING == x

        @pl.when(stays)
        def _():
            y_stays(j, e).start()

        @pl.when(jnp.logical_not(stays))
        def _():
            y_copy(j, e).start()

    def block_copy(src, halo, d, r, send, recv):
        return pltpu.make_async_remote_copy(
            src, halo.at[1 - d, r], send.at[d], recv.at[1 - d, r], device_id={"row": near_block[d]}, device_id_type=MESH
        )

    def yh_copy(d, r):
        return block_copy(y_in.at[r, d * (2 * RING - 1)], y_halo, d, r, yh_send, yh_recv)

    def u_copy(d, r):
        return block_copy(u_out.at[d, r], u_halo, d, r, u_send, u_recv)

    def f_copy(o, c):
        to = (x + o) % RING
        return pltpu.make_async_remote_copy(
            f_out.at[2 * to + c], f_in.at[RING * k + x], f_send.at[0], f_recv.at[0],
            device_id={"col": c, "row": first + to}, device_id_type=MESH,
        )

    def f_stays():
        return pltpu.make_async_copy(f_out.at[2 * x + k], f_in.at[RING * k + x], f_recv.at[0])

    def w_copy(i):
        return pltpu.make_async_copy(w_hbm[i], w_refs[i], w_sem.at[i])

    def b_copy(i):
        return pltpu.make_async_copy(b_hbm[i], b_all.at[i], b_sem.at[0])

    for d in range(2):
        edge_load(d).start()
    for i in range(half):
        own_copy(turn(i, x)).start()
        if i == 0:
            w_copy(0).start()
    for i in range(6):
        b_copy(i).start()

    for (stride, _, _), s in zip(LAYERS, s_refs):
        w = s.shape[-2] - 3 * PAD
        edge = jnp.zeros(s.shape[:-2] + (PAD, LANES), F32)
        s[..., pl.ds(0, PAD), :] = edge
        s[..., pl.ds(PAD + w, PAD), :] = edge
    for d in range(2):
        @pl.when(jnp.logical_not(has[d]))
        def _():
            xhalo[d] = jnp.zeros(xhalo.shape[1:], BF16)

        @pl.when(jnp.logical_not(has_block[d]))
        def _():
            y_halo[d] = jnp.zeros(y_halo.shape[1:], BF16)
            u_halo[d] = jnp.zeros(u_halo.shape[1:], BF16)

    settle(xedge, load_sem.at[0])
    count = 2 * RING - 1
    for d in range(2):
        count = count + 2 * crosses[d].astype(jnp.int32) + has_block[d].astype(jnp.int32)
    pl.semaphore_wait(barrier, count)

    for i in range(half):
        part_copy(turn(i, x)).start()
        for d in range(2):
            @pl.when(has[d])
            def _():
                for c in range(2):
                    edge_copy(d, c, turn(i, (x + 2 * d - 1) % RING)).start()
    for i in range(1, 6):
        w_copy(i).start()

    def keep(i, v, r):
        s = s_refs[i]
        w = s.shape[-2] - 3 * PAD
        for h in range(v.shape[-1] // LANES):
            s[h, pl.ds(r, v.shape[0]), pl.ds(PAD, w), :] = v[:, :, h * LANES : (h + 1) * LANES]

    def spread(i, rows, a):
        stride, taps, _ = LAYERS[i]
        s = s_refs[i]
        w = (s.shape[-2] - 3 * PAD) // stride
        tiles = [(q, h) for q in range(taps) for h in range(s.shape[0])]
        for r in rows:
            for t in range(0, len(tiles), 2):
                pair = []
                for q, h in tiles[t : t + 2]:
                    at = pl.ds(PAD - 1 + q, w) if stride == 1 else pl.ds(PAD - 1 + q, w, stride=2)
                    pair.append(s[h, r, at, :])
                v = jnp.concatenate(pair, axis=-1).astype(BF16)
                lanes = pl.ds(t * LANES, 2 * LANES)
                if stride == 1:
                    a[r, :, lanes] = v
                else:
                    a[r % 2, r // 2, :, lanes] = v

    def product(i, a, o, n):
        stride, taps, _ = LAYERS[i]
        sums = [None, None]
        for p in range(taps):
            left = a[pl.ds(o + p, n)] if stride == 1 else a[p % 2, pl.ds(o + p // 2, n)]
            _, w, depth = left.shape
            left = left.reshape(n * w, depth)
            for b in range(0, depth, 2 * LANES):
                piece = jnp.dot(left[:, b : b + 2 * LANES], w_refs[i][p, pl.ds(b, 2 * LANES)], preferred_element_type=F32)
                at = int(i >= 4 and 2 * (p * depth + b) >= taps * depth)
                sums[at] = piece if sums[at] is None else sums[at] + piece
        acc = sums[0] if sums[1] is None else sums[0] + jnp.where(k >= 0, sums[1], 0.0)
        v = jnp.maximum(acc + b_all[i], 0.0)
        return v.reshape(n, w, v.shape[-1])

    def inside(v, d):
        return jnp.where(has_block[d], v, 0.0)

    def first_step(i):
        j = turn(i, x)
        settle(ximg.at[j], in_sem.at[j])
        for d in range(2):
            @pl.when(has[d])
            def _():
                settle(xhalo.at[d, j], edge_recv.at[d, j])
        s = s_refs[0]
        for c in range(2):
            at = pl.ds(PAD + c * col_half, col_half)
            s[0, 0, at, :] = xhalo[0, j, c].astype(F32)
            s[0, pl.ds(1, tile_rows), at, :] = ximg[j, c].astype(F32)
            s[0, tile_rows + 1, at, :] = xhalo[1, j, c].astype(F32)
        spread(0, range(tile_rows + 2), a_refs[0])
        for e in range(2):
            y_out[j, e] = product(0, a_refs[0], e * y_part, y_part).astype(BF16)
        edge = x // (RING - 1)
        y_leaves(j, edge)

        @pl.when(i >= half - RING)
        def _():
            y_leaves(turn(i - half + RING, x), 1 - edge)

    def forward(r):
        for d in range(2):
            settle(y_in.at[r, d * (2 * RING - 1)], y_recv.at[r, d])

            @pl.when(has_block[d])
            def _():
                yh_copy(d, r).start()

    def second_step(r):
        a1, a2, a3 = a_refs[1], a_refs[2], a_refs[3].at[r]
        own = RING * y_rows
        settle(y_in.at[r, pl.ds(1, 2 * RING - 2)], y_recv.at[r, 2])
        for place in range(2 * RING):
            keep(1, y_in[r, place].astype(F32), 2 + place * y_part)
        n = 3
        for o in range(n, own + 2 - n, n):
            spread(1, range(o if o == n else o + 2, o + n + 2), a1)
            keep(2, product(1, a1, o, n), o)
            spread(2, range(o, o + n), a2)
        for d in range(2):
            @pl.when(has_block[d])
            def _():
                settle(y_halo.at[d, r], yh_recv.at[d, r])
        keep(1, y_halo[0, r].astype(F32), 0)
        keep(1, y_halo[1, r].astype(F32), 2 + own)
        low = own + 2 - n
        spread(1, range(0, n), a1)
        v = product(1, a1, 0, n)
        spread(1, range(low + 2, own + 4), a1)
        u = product(1, a1, low, n)
        keep(2, inside(v[:1], 0), 0)
        keep(2, v[1:], 1)
        spread(2, range(n), a2)
        keep(2, u[: n - 1], low)
        keep(2, inside(u[n - 1 :], 1), own + 1)
        spread(2, range(low, low + n), a2)
        u_rows = own // 2
        depth = u_halo.shape[2]
        n = u_rows // 2
        for e in range(2):
            v = product(2, a2, e * n, n)
            u_out[e, r] = v.astype(BF16)
            keep(3, v, depth + e * n)
        for d in range(2):
            @pl.when(has_block[d])
            def _():
                u_copy(d, r).start()
        spread(3, range(depth, depth + u_rows), a3)

    def third_step(r):
        a3, a4, a5 = a_refs[3].at[r], a_refs[4], a_refs[5]
        depth = u_halo.shape[2]
        u_rows = RING * y_rows // 2
        n = (u_rows - 2) // 2
        for o in (depth, depth + n):
            keep(4, product(3, a3, o, n), o)
        spread(4, range(depth, depth + u_rows - 2), a4)
        for d in range(2):
            @pl.when(has_block[d])
            def _():
                settle(u_halo.at[d, r], u_recv.at[d, r])
        for d, o in ((0, 0), (1, depth + u_rows)):
            keep(3, u_halo[d, r].astype(F32), o)
            spread(3, range(o, o + depth), a3)
        low = depth + u_rows - 2
        v = product(3, a3, 0, depth)
        keep(4, inside(v[: depth - 1], 0), 0)
        keep(4, v[depth - 1 :], depth - 1)
        v = product(3, a3, low, depth)
        keep(4, v[:1], low)
        keep(4, inside(v[1:], 1), low + 1)
        for o in (0, low):
            spread(4, range(o, o + depth), a4)
        f_rows = u_rows // 2
        v = product(4, a4, 0, f_rows + 2)
        keep(5, inside(v[:1], 0), 0)
        keep(5, v[1 : 1 + f_rows], 1)
        keep(5, inside(v[1 + f_rows :], 1), 1 + f_rows)
        spread(5, range(f_rows + 2), a5)
        v = product(5, a5, 0, f_rows)
        w = v.shape[1] // 2
        for t in range(f_rows):
            for c in range(2):
                f_out[2 * t + c, r] = v[t, c * w : (c + 1) * w].astype(BF16)

    def ready(i):
        w_copy(i).wait()

    settle(b_all, b_sem.at[0])
    ready(0)
    pl.loop(0, half)(first_step)
    for i in range(half - RING, half):
        y_leaves(turn(i, x), 1 - x // (RING - 1))
    ready(1)
    ready(2)
    for r in range(per):
        forward(r)
    pl.loop(0, per)(second_step)
    for i in (3, 4, 5):
        ready(i)
    pl.loop(0, per)(third_step)

    for o in (2, 1, 3, 0):
        for c in range(2):
            if o:
                f_copy(o, c).start()
            else:
                @pl.when(k == c)
                def _():
                    f_stays().start()

                @pl.when(k != c)
                def _():
                    f_copy(0, c).start()

    settle(ximg.at[:, 0], part_send.at[0])
    settle(y_out.at[pl.ds(0, half - per)], y_send.at[0])
    for d in range(2):
        @pl.when(has[d])
        def _():
            settle(xedge.at[d], edge_send.at[d])

        @pl.when(has_block[d])
        def _():
            settle(y_halo.at[d], yh_send.at[d])
            settle(u_out.at[d], u_send.at[d])
    settle(f_out.at[pl.ds(0, 2 * RING - 1)], f_send.at[0])
    settle(f_in, f_recv.at[0])
    for c in range(2):
        for src in range(RING):
            for r in range(per):
                out_ref[c * half + r * RING + src, 0] = f_in[c * RING + src, r]


def solution(mesh):
    row_len = mesh.shape["row"]

    def local_encoder(images, *params):
        n_img, rows, col_half, c_in = images.shape
        half = n_img // 2
        per = half // RING
        weights, biases = params[0::2], params[1::2]
        c_out = weights[0].shape[-1]
        args = [images]
        for w, b in zip(weights, biases):
            args += [w.reshape(w.shape[0], w.shape[1] * w.shape[2], c_out), b.reshape(1, c_out)]
        args = [pltpu.with_memory_space_constraint(v, pltpu.HBM) for v in args]

        y_rows, u_rows, f_rows = rows // 2, RING * rows // 4, RING * rows // 8
        width = 2 * col_half
        depth1, depth3 = LAYERS[1][2], LAYERS[3][2]
        vmem, dma = pltpu.VMEM, pltpu.SemaphoreType.DMA
        scratch = [
            vmem((half, 2, rows, col_half, c_in), BF16),
            vmem((2, n_img, col_half, c_in), BF16),
            vmem((2, half, 2, col_half, c_in), BF16),
            vmem((half, 2, y_rows // 2, width // 2, c_out), BF16),
            vmem((per, 2 * RING, y_rows // 2, width // 2, c_out), BF16),
            vmem((2, per, depth1, width // 2, c_out), BF16),
            vmem((2, per, depth3, width // 4, c_out), BF16),
            vmem((2, per, depth3, width // 4, c_out), BF16),
            vmem((2 * f_rows, per, width // 16, c_out), BF16),
            vmem((2 * RING, per, width // 16, c_out), BF16),
        ]
        scratch += [vmem(w.shape, BF16) for w in args[1::2]]
        scratch += [vmem((6, 1, c_out), F32)]
        held, spans = [], (rows, RING * y_rows, RING * y_rows, u_rows, u_rows, f_rows)
        for i, (stride, taps, ext) in enumerate(LAYERS):
            chan = c_in if i == 0 else c_out
            total, w = spans[i] + 2 * ext, width // (1, 2, 2, 4, 4, 8)[i]
            shape = (total, w, taps * chan) if stride == 1 else (2, total // 2, w // 2, taps * chan)
            scratch.append(vmem((per,) + shape if i == 3 else shape, BF16))
            held.append(vmem((chan // LANES, total, w + 3 * PAD, LANES), F32))
        scratch += held
        scratch += [dma((6,)), dma((1,)), dma((half,)), dma((1,)), dma((1,)), dma((2,)), dma((2, half))]
        scratch += [dma((1,)), dma((per, 3))] + [dma((2,)), dma((2, per))] * 2 + [dma((1,)), dma((1,))]

        any_spec = pl.BlockSpec(memory_space=pl.ANY)
        return pl.pallas_call(
            functools.partial(kernel, half, row_len),
            out_shape=jax.ShapeDtypeStruct((n_img, rows // 8, col_half // 8, c_out), BF16),
            in_specs=[any_spec] * len(args),
            out_specs=pl.BlockSpec(memory_space=pltpu.VMEM),
            scratch_shapes=scratch,
            compiler_params=pltpu.CompilerParams(collective_id=0, has_side_effects=True, vmem_limit_bytes=53 * 1024 * 1024),
            name="encoder",
        )(*args)

    tile_spec = P("batch", "row", "col", None)
    return jax.shard_map(local_encoder, mesh=mesh, in_specs=(tile_spec,) + (P(),) * 12, out_specs=tile_spec, check_vma=False)
```

time: 41.8 us -> 38.4 us (0.919)
  Pallas kernels: 40.2 us -> 37.6 us
  local copies, waits for them, and re-layouts: 1.47 us -> 0.63 us
    pallas_call x1, Pallas kernels: 40.2 us -> 37.6 us  [local_encoder(): pl.pallas_call(functools.partial(kernel, half, row_len), out_shape=jax.Sh...]
    unnamed x1, local copies, waits for them, and re-layouts: 1.47 us -> 0.63 us
where the time goes in v4:
time: 38.4 us; the launch traced here: 38.3 us
  Pallas kernels  37.6 us (98%)
  local copies, waits for them, and re-layouts  0.63 us (2%)
    pallas_call x1, Pallas kernels, local_encoder(): pl.pallas_call(functools.partial(kernel, half, row_len), out_shape=jax.Sh...  37.6 us

profile of v4, /device:TPU:97, one launch (start us, length us, event | category | flops | bytes accessed | tf_op | source)
XLA Modules:
  0.0 38.3 jit_solution(680762830065925154)
XLA Ops:
  0.0 37.6 %encoder.1 = bf16[16,1,8,256]{3,2,1,0:T(8,128)(2,1)S(1)} custom-call(bf16[16,8,64,128]{3,2,1,0:T(8,128)(2,1)} %refs_0_.1, bf16[4,512,256]{2,1,0:T(8,128)(2,1)} %bitcast.17, f32[1,256]{1,0:T(1,128)} %bitcast.18, bf16[3,768,256]{2,1,0:T(8,128)(2,1)} %bitcast.14, f32[1,256]{1,0:T(1,128)} %bitcast.19, bf16[4,1024,256]{2,1,0:T(8,128)(2,1)} %bitcast.12, ...), custom_call_target="tpu_custom_call" | custom-call | tf_op jit(solution)/shard_map/encoder/pallas_call | solution.py:417
  37.6 0.6 %copy.15 = bf16[16,1,8,256]{3,2,1,0:T(8,128)(2,1)} copy(bf16[16,1,8,256]{3,2,1,0:T(8,128)(2,1)S(1)} %encoder.1) | data formatting | bytes 131072

commit v5 on v4

--- a/solution.py
+++ b/solution.py
@@ -112,8 +112,11 @@
     def yh_copy(d, r):
         return block_copy(y_in.at[r, d * (2 * RING - 1)], y_halo, d, r, yh_send, yh_recv)
 
-    def u_copy(d, r):
-        return block_copy(u_out.at[d, r], u_halo, d, r, u_send, u_recv)
+    def u_copy(d, r, o):
+        return pltpu.make_async_remote_copy(
+            u_out.at[d, r, pl.ds(o, 2)], u_halo.at[1 - d, r, pl.ds(o, 2)], u_send.at[d], u_recv.at[1 - d, r],
+            device_id={"row": near_block[d]}, device_id_type=MESH,
+        )
 
     def f_copy(o, c):
         to = (x + o) % RING
@@ -195,16 +198,17 @@
                 else:
                     a[r % 2, r // 2, :, lanes] = v
 
-    def product(i, a, o, n):
+    def product(i, a, *spans):
         stride, taps, _ = LAYERS[i]
         sums = [None, None]
         for p in range(taps):
-            left = a[pl.ds(o + p, n)] if stride == 1 else a[p % 2, pl.ds(o + p // 2, n)]
-            _, w, depth = left.shape
+            parts = [a[pl.ds(o + p, n)] if stride == 1 else a[p % 2, pl.ds(o + p // 2, n)] for o, n in spans]
+            left = parts[0] if len(parts) == 1 else jnp.concatenate(parts, axis=0)
+            n, w, depth = left.shape
             left = left.reshape(n * w, depth)
             for b in range(0, depth, 2 * LANES):
                 piece = jnp.dot(left[:, b : b + 2 * LANES], w_refs[i][p, pl.ds(b, 2 * LANES)], preferred_element_type=F32)
-                at = int(i >= 4 and 2 * (p * depth + b) >= taps * depth)
+                at = int(i in (2, 4, 5) and 2 * (p * depth + b) >= taps * depth)
                 sums[at] = piece if sums[at] is None else sums[at] + piece
         acc = sums[0] if sums[1] is None else sums[0] + jnp.where(k >= 0, sums[1], 0.0)
         v = jnp.maximum(acc + b_all[i], 0.0)
@@ -228,7 +232,7 @@
             s[0, tile_rows + 1, at, :] = xhalo[1, j, c].astype(F32)
         spread(0, range(tile_rows + 2), a_refs[0])
         for e in range(2):
-            y_out[j, e] = product(0, a_refs[0], e * y_part, y_part).astype(BF16)
+            y_out[j, e] = product(0, a_refs[0], (e * y_part, y_part)).astype(BF16)
         edge = x // (RING - 1)
         y_leaves(j, edge)
 
@@ -250,11 +254,25 @@
         settle(y_in.at[r, pl.ds(1, 2 * RING - 2)], y_recv.at[r, 2])
         for place in range(2 * RING):
             keep(1, y_in[r, place].astype(F32), 2 + place * y_part)
-        n = 3
-        for o in range(n, own + 2 - n, n):
-            spread(1, range(o if o == n else o + 2, o + n + 2), a1)
-            keep(2, product(1, a1, o, n), o)
-            spread(2, range(o, o + n), a2)
+        n = 2
+        m = (own - 6) // 2
+        spread(1, range(4, 6), a1)
+        for o, rows in ((4, m), (4 + m, m), (n, n), (own - n, n)):
+            new = range(o, o + n) if o == n else range(o + n, o + n + rows)
+            spread(1, new, a1)
+            keep(2, product(1, a1, (o, rows)), o)
+            spread(2, range(o, o + rows), a2)
+        u_rows = own // 2
+        depth = u_halo.shape[2]
+        mid = product(2, a2, (2, u_rows - 4))
+        u_out[0, r, pl.ds(2, depth - 2)] = mid[: depth - 2].astype(BF16)
+        u_out[1, r, pl.ds(0, depth - 2)] = mid[depth - 2 :].astype(BF16)
+        keep(3, mid, depth + 2)
+        for d in range(2):
+            @pl.when(has_block[d])
+            def _():
+                u_copy(d, r, 2 - 2 * d).start()
+
         for d in range(2):
             @pl.when(has_block[d])
             def _():
@@ -263,26 +281,24 @@
         keep(1, y_halo[1, r].astype(F32), 2 + own)
         low = own + 2 - n
         spread(1, range(0, n), a1)
-        v = product(1, a1, 0, n)
+        v = product(1, a1, (0, n))
         spread(1, range(low + 2, own + 4), a1)
-        u = product(1, a1, low, n)
+        u = product(1, a1, (low, n))
         keep(2, inside(v[:1], 0), 0)
         keep(2, v[1:], 1)
         spread(2, range(n), a2)
         keep(2, u[: n - 1], low)
         keep(2, inside(u[n - 1 :], 1), own + 1)
         spread(2, range(low, low + n), a2)
-        u_rows = own // 2
-        depth = u_halo.shape[2]
-        n = u_rows // 2
-        for e in range(2):
-            v = product(2, a2, e * n, n)
-            u_out[e, r] = v.astype(BF16)
-            keep(3, v, depth + e * n)
+        rim = product(2, a2, (0, 2), (u_rows - 2, 2))
+        u_out[0, r, pl.ds(0, 2)] = rim[:2].astype(BF16)
+        u_out[1, r, pl.ds(depth - 2, 2)] = rim[2:].astype(BF16)
         for d in range(2):
             @pl.when(has_block[d])
             def _():
-                u_copy(d, r).start()
+                u_copy(d, r, 2 * d).start()
+        keep(3, rim[:2], depth)
+        keep(3, rim[2:], depth + u_rows - 2)
         spread(3, range(depth, depth + u_rows), a3)
 
     def third_step(r):
@@ -291,7 +307,7 @@
         u_rows = RING * y_rows // 2
         n = (u_rows - 2) // 2
         for o in (depth, depth + n):
-            keep(4, product(3, a3, o, n), o)
+            keep(4, product(3, a3, (o, n)), o)
         spread(4, range(depth, depth + u_rows - 2), a4)
         for d in range(2):
             @pl.when(has_block[d])
@@ -301,21 +317,21 @@
             keep(3, u_halo[d, r].astype(F32), o)
             spread(3, range(o, o + depth), a3)
         low = depth + u_rows - 2
-        v = product(3, a3, 0, depth)
+        v = product(3, a3, (0, depth))
         keep(4, inside(v[: depth - 1], 0), 0)
         keep(4, v[depth - 1 :], depth - 1)
-        v = product(3, a3, low, depth)
+        v = product(3, a3, (low, depth))
         keep(4, v[:1], low)
         keep(4, inside(v[1:], 1), low + 1)
         for o in (0, low):
             spread(4, range(o, o + depth), a4)
         f_rows = u_rows // 2
-        v = product(4, a4, 0, f_rows + 2)
+        v = product(4, a4, (0, f_rows + 2))
         keep(5, inside(v[:1], 0), 0)
         keep(5, v[1 : 1 + f_rows], 1)
         keep(5, inside(v[1 + f_rows :], 1), 1 + f_rows)
         spread(5, range(f_rows + 2), a5)
-        v = product(5, a5, 0, f_rows)
+        v = product(5, a5, (0, f_rows))
         w = v.shape[1] // 2
         for t in range(f_rows):
             for c in range(2):

time: 38.4 us -> 37.7 us (0.982)
  Pallas kernels: 37.6 us -> 36.9 us
    pallas_call x1, Pallas kernels: 37.6 us -> 36.9 us  [local_encoder(): pl.pallas_call(functools.partial(kernel, half, row_len), out_shape=jax.Sh...]
where the time goes in v5:
time: 37.7 us; the launch traced here: 37.5 us
  Pallas kernels  36.9 us (98%)
  local copies, waits for them, and re-layouts  0.63 us (2%)
    pallas_call x1, Pallas kernels, local_encoder(): pl.pallas_call(functools.partial(kernel, half, row_len), out_shape=jax.Sh...  36.9 us

profile of v5, /device:TPU:97, one launch (start us, length us, event | category | flops | bytes accessed | tf_op | source)
XLA Modules:
  0.0 37.5 jit_solution(8726906199518948139)
XLA Ops:
  0.0 36.9 %encoder.1 = bf16[16,1,8,256]{3,2,1,0:T(8,128)(2,1)S(1)} custom-call(bf16[16,8,64,128]{3,2,1,0:T(8,128)(2,1)} %refs_0_.1, bf16[4,512,256]{2,1,0:T(8,128)(2,1)} %bitcast.17, f32[1,256]{1,0:T(1,128)} %bitcast.18, bf16[3,768,256]{2,1,0:T(8,128)(2,1)} %bitcast.14, f32[1,256]{1,0:T(1,128)} %bitcast.19, bf16[4,1024,256]{2,1,0:T(8,128)(2,1)} %bitcast.12, ...), custom_call_target="tpu_custom_call" | custom-call | tf_op jit(solution)/shard_map/encoder/pallas_call | solution.py:433
  36.9 0.6 %copy.15 = bf16[16,1,8,256]{3,2,1,0:T(8,128)(2,1)} copy(bf16[16,1,8,256]{3,2,1,0:T(8,128)(2,1)S(1)} %encoder.1) | data formatting | bytes 131072

commit v6 on v5

--- a/solution.py
+++ b/solution.py
@@ -118,15 +118,15 @@
             device_id={"row": near_block[d]}, device_id_type=MESH,
         )
 
-    def f_copy(o, c):
+    def f_copy(o, c, r):
         to = (x + o) % RING
         return pltpu.make_async_remote_copy(
-            f_out.at[2 * to + c], f_in.at[RING * k + x], f_send.at[0], f_recv.at[0],
+            f_out.at[2 * to + c, r], f_in.at[RING * k + x, r], f_send.at[0], f_recv.at[0],
             device_id={"col": c, "row": first + to}, device_id_type=MESH,
         )
 
-    def f_stays():
-        return pltpu.make_async_copy(f_out.at[2 * x + k], f_in.at[RING * k + x], f_recv.at[0])
+    def f_stays(r):
+        return pltpu.make_async_copy(f_out.at[2 * x + k, r], f_in.at[RING * k + x, r], f_recv.at[0])
 
     def w_copy(i):
         return pltpu.make_async_copy(w_hbm[i], w_refs[i], w_sem.at[i])
@@ -337,6 +337,19 @@
             for c in range(2):
                 f_out[2 * t + c, r] = v[t, c * w : (c + 1) * w].astype(BF16)
 
+        for o in (2, 1, 3, 0):
+            for c in range(2):
+                if o:
+                    f_copy(o, c, r).start()
+                else:
+                    @pl.when(k == c)
+                    def _():
+                        f_stays(r).start()
+
+                    @pl.when(k != c)
+                    def _():
+                        f_copy(0, c, r).start()
+
     def ready(i):
         w_copy(i).wait()
 
@@ -353,19 +366,6 @@
     for i in (3, 4, 5):
         ready(i)
     pl.loop(0, per)(third_step)
-
-    for o in (2, 1, 3, 0):
-        for c in range(2):
-            if o:
-                f_copy(o, c).start()
-            else:
-                @pl.when(k == c)
-                def _():
-                    f_stays().start()
-
-                @pl.when(k != c)
-                def _():
-                    f_copy(0, c).start()
 
     settle(ximg.at[:, 0], part_send.at[0])
     settle(y_out.at[pl.ds(0, half - per)], y_send.at[0])

time: 37.7 us -> 37.6 us (level)
  no operation moved by 1% of the time
where the time goes in v6:
time: 37.6 us; the launch traced here: 37.4 us
  Pallas kernels  36.8 us (98%)
  local copies, waits for them, and re-layouts  0.63 us (2%)
    pallas_call x1, Pallas kernels, local_encoder(): pl.pallas_call(functools.partial(kernel, half, row_len), out_shape=jax.Sh...  36.8 us

profile of v6, /device:TPU:97, one launch (start us, length us, event | category | flops | bytes accessed | tf_op | source)
XLA Modules:
  0.0 37.4 jit_solution(782452562824777230)
XLA Ops:
  0.0 36.8 %encoder.1 = bf16[16,1,8,256]{3,2,1,0:T(8,128)(2,1)S(1)} custom-call(bf16[16,8,64,128]{3,2,1,0:T(8,128)(2,1)} %refs_0_.1, bf16[4,512,256]{2,1,0:T(8,128)(2,1)} %bitcast.17, f32[1,256]{1,0:T(1,128)} %bitcast.18, bf16[3,768,256]{2,1,0:T(8,128)(2,1)} %bitcast.14, f32[1,256]{1,0:T(1,128)} %bitcast.19, bf16[4,1024,256]{2,1,0:T(8,128)(2,1)} %bitcast.12, ...), custom_call_target="tpu_custom_call" | custom-call | tf_op jit(solution)/shard_map/encoder/pallas_call | solution.py:433
  36.8 0.6 %copy.15 = bf16[16,1,8,256]{3,2,1,0:T(8,128)(2,1)} copy(bf16[16,1,8,256]{3,2,1,0:T(8,128)(2,1)S(1)} %encoder.1) | data formatting | bytes 131072
